TPU v7x, 32 devices: a whole 2x2x4 slice. The times are simulated.
32 devices in a mesh: row: 4 (over x, core), col: 8 (over z, y).
Axes of the slice: x: 2, y: 2, z: 4, core: 2. Of those that a mesh axis runs over, the one named last changes fastest.
Arguments:
- w_rec: bfloat16 [2, 4096, 4, 4096], P(None, 'row', None, 'col'), may hold values from -0.09375 to 0.09375
- w_in: bfloat16 [2, 4096, 4, 4096], P(None, 'row', None, 'col'), may hold values from -0.09375 to 0.09375
- gate_pre: float32 [2, 6, 64, 4, 4096], P(None, None, None, None, 'col'), may hold values from -8 to 8, as said below
- cells: float32 [2, 7, 64, 4096], P(None, None, None, 'col'), may hold values from -6 to 6
- layer_in: bfloat16 [2, 6, 64, 4096], P(None, None, None, 'row'), may hold values from -1 to 1
- h_prev: bfloat16 [2, 6, 64, 4096], P(None, None, None, 'row'), may hold values from -1 to 1
- top_grad: float32 [6, 64, 4096], P(None, None, 'col'), may hold values from -40 to 40
Outputs:
- w_rec_grad: bfloat16 [2, 4096, 4, 4096], P(None, 'row', None, 'col')
- w_in_grad: bfloat16 [2, 4096, 4, 4096], P(None, 'row', None, 'col')
- input_grad: float32 [6, 64, 4096], P(None, None, 'col')
Inputs may be any that keep to these rules, and one draw needn't show every extreme that they name: `gate_pre`: dimension 3 holds the input, forget, candidate and output gates in that order.
All inputs are finite; a program needn't handle non-finite values.
Results may differ from a plain program's by a relative error of at most 0.0051.
Values sent between devices are 32-bit elements; how exact they have to be, the bound alone decides.
No kernel may reach another device: no remote copies, remote signals or barrier semaphores. Data moves between devices by JAX's collectives and lax.ppermute only.
A program may use at most 128 MiB of HBM per device.

v0:
```python
import functools

import jax
import jax.numpy as jnp
from jax import lax
from jax.experimental import pallas as pl
from jax.experimental.pallas import tpu as pltpu
from jax.sharding import PartitionSpec as P

NT = (((1,), (1,)), ((), ()))
TN = (((0,), (0,)), ((), ()))
VMEM_LIMIT = 60 * 1024 * 1024
CUT = 2


def step_kernel(plan, products, *refs):
    refs = list(refs)
    live = []
    for entry in plan:
        need = ["gate", "prev", "now"] + [name for name in ("carry", "top", "got") if entry[name]]
        live.append({name: refs.pop(0) for name in need})
    weights = [[refs.pop(0) for _ in terms] for terms in products]
    for entry in plan:
        if entry["alias"]:
            refs.pop(0)
    outs = []
    for entry in plan:
        out = {"grads": refs.pop(0)}
        if entry["send"]:
            out["carry"] = refs.pop(0)
        outs.append(out)

    @pl.when(pl.program_id(0) == 0)
    def _():
        for entry, ins, out in zip(plan, live, outs):
            units = ins["prev"].shape[-1]
            gate = ins["gate"]
            in_gate = jax.nn.sigmoid(gate[0, 0, :, 0, :])
            forget = jax.nn.sigmoid(gate[0, 0, :, 1, :])
            cand_gate = jnp.tanh(gate[0, 0, :, 2, :])
            out_gate = jax.nn.sigmoid(gate[0, 0, :, 3, :])
            tanh_cell = jnp.tanh(ins["now"][0, 0])
            hid_grad = None
            if entry["top"]:
                hid_grad = ins["top"][0]
            if entry["got"]:
                batch = out["grads"].shape[0]
                got = ins["got"][pl.ds(entry["at"] * batch, batch), :]
                hid_grad = got if hid_grad is None else hid_grad + got
            cell_grad = hid_grad * out_gate * (1.0 - tanh_cell * tanh_cell)
            if entry["carry"]:
                cell_grad = cell_grad + ins["carry"][...]
            parts = (
                cell_grad * cand_gate * in_gate * (1.0 - in_gate),
                cell_grad * ins["prev"][0, 0] * forget * (1.0 - forget),
                cell_grad * in_gate * (1.0 - cand_gate * cand_gate),
                hid_grad * tanh_cell * out_gate * (1.0 - out_gate),
            )
            for k, part in enumerate(parts):
                out["grads"][:, k * units : (k + 1) * units] = part.astype(jnp.bfloat16)
            if entry["send"]:
                out["carry"][...] = cell_grad * forget

    if products:
        partial = refs.pop(0)
        for slot, (terms, w_refs) in enumerate(zip(products, weights)):
            total = None
            for which, w_ref in zip(terms, w_refs):
                grads = outs[which]["grads"]
                term = lax.dot_general(
                    grads[...], w_ref[...], NT, preferred_element_type=jnp.float32
                )
                total = term if total is None else total + term
            batch = total.shape[0]
            partial[0, slot * batch : (slot + 1) * batch, :] = total


def run_step(plan, products, gate_pre, cells, top_grad, got, carry, store):
    steps, batch, units = top_grad.shape
    tile = min(256, units)
    ins, in_specs, out_shape, out_specs, aliases = [], [], [], [], {}

    def take(array, block, index):
        ins.append(array)
        in_specs.append(pl.BlockSpec(block, lambda i: index))

    for entry in plan:
        l, t = entry["layer"], entry["step"]
        take(gate_pre, (1, 1, batch, 4, units), (l, t, 0, 0, 0))
        take(cells, (1, 1, batch, units), (l, t, 0, 0))
        take(cells, (1, 1, batch, units), (l, t + 1, 0, 0))
        if entry["carry"]:
            take(carry[l], (batch, units), (0, 0))
        if entry["top"]:
            take(top_grad, (1, batch, units), (t, 0, 0))
        if entry["got"]:
            take(got, got.shape, (0, 0))
    rows = None
    for terms in products:
        for _, weight in terms:
            rows = weight.shape[0]
            ins.append(weight)
            in_specs.append(pl.BlockSpec((tile, weight.shape[1]), lambda i: (i, 0)))
    for entry in plan:
        l, t = entry["layer"], entry["step"]
        if entry["alias"]:
            aliases[len(ins)] = len(out_shape)
            ins.append(store[l])
            in_specs.append(pl.BlockSpec(memory_space=pl.ANY))
        out_shape.append(jax.ShapeDtypeStruct((steps * batch, 4 * units), jnp.bfloat16))
        out_specs.append(pl.BlockSpec((batch, 4 * units), lambda i, t=t: (t, 0)))
        if entry["send"]:
            out_shape.append(jax.ShapeDtypeStruct((batch, units), jnp.float32))
            out_specs.append(pl.BlockSpec((batch, units), lambda i: (0, 0)))
    grid = 1
    flops = 0
    if products:
        grid = rows // tile
        per = units // tile
        count = len(products) * batch
        out_shape.append(jax.ShapeDtypeStruct((rows // units, count, units), jnp.float32))
        out_specs.append(pl.BlockSpec((1, count, tile), lambda i: (i // per, 0, i % per)))
        flops = sum(len(terms) for terms in products) * 2 * batch * rows * 4 * units
    outs = pl.pallas_call(
        functools.partial(step_kernel, plan, [[which for which, _ in terms] for terms in products]),
        grid=(grid,),
        out_shape=out_shape,
        in_specs=in_specs,
        out_specs=out_specs,
        input_output_aliases=aliases,
        compiler_params=pltpu.CompilerParams(vmem_limit_bytes=VMEM_LIMIT),
        cost_estimate=pl.CostEstimate(
            flops=flops + 1000, bytes_accessed=flops // batch + 10**6, transcendentals=0
        ),
    )(*ins)
    outs = list(outs)
    for entry in plan:
        store[entry["layer"]] = outs.pop(0)
        if entry["send"]:
            carry[entry["layer"]] = outs.pop(0)
    return outs.pop(0) if products else None


def grads_kernel(scale_ref, rec_ref, in_ref, flat_ref, rec_out, in_out, held):
    scale = scale_ref[0, 0]
    units = rec_out.shape[-1]
    for saved, out in ((rec_ref, rec_out), (in_ref, in_out)):
        for k in range(4):
            raw = lax.dot_general(
                saved[0],
                flat_ref[:, k * units : (k + 1) * units],
                TN,
                preferred_element_type=jnp.float32,
            )
            held[:, k, :] = raw * scale
        out[0] = held[...].astype(jnp.bfloat16)


def grads_kernel_keep(scale_ref, rec_ref, in_ref, flat_ref, a, b, rec_out, in_out, held):
    grads_kernel(scale_ref, rec_ref, in_ref, flat_ref, rec_out, in_out, held)


def layer_grads(layer, scale, saved_rec, saved_in, flat, before):
    layers, count, rows = saved_rec.shape
    units = flat.shape[1] // 4
    tile = min(256, rows)
    block = pl.BlockSpec((1, count, tile), lambda j: (layer, 0, j))
    kept = pl.BlockSpec(memory_space=pl.ANY)
    out = pl.BlockSpec((1, tile, 4, units), lambda j: (layer, j, 0, 0))
    return pl.pallas_call(
        grads_kernel_keep if before else grads_kernel,
        grid=(rows // tile,),
        out_shape=[jax.ShapeDtypeStruct((layers, rows, 4, units), jnp.bfloat16)] * 2,
        in_specs=[
            pl.BlockSpec(memory_space=pltpu.SMEM),
            block,
            block,
            pl.BlockSpec((count, 4 * units), lambda j: (0, 0)),
        ]
        + [kept] * len(before),
        out_specs=[out, out],
        scratch_shapes=[pltpu.VMEM((tile, 4, units), jnp.float32)],
        input_output_aliases={4: 0, 5: 1} if before else {},
        compiler_params=pltpu.CompilerParams(vmem_limit_bytes=VMEM_LIMIT),
        cost_estimate=pl.CostEstimate(
            flops=2 * 2 * count * rows * 4 * units,
            bytes_accessed=2 * rows * 4 * units * 2,
            transcendentals=0,
        ),
    )(scale, saved_rec, saved_in, flat, *before)


def swap(partial):
    cols = lax.axis_size("col")
    ratio, count, units = partial.shape
    pieces = partial.reshape(cols, ratio * count // cols, units)
    return lax.all_to_all(pieces, "col", 0, 0, tiled=True)


def place(mine):
    rows = lax.axis_size("row")
    cols = lax.axis_size("col")
    ratio = cols // rows
    moves = [
        (r * cols + k, (k % rows) * cols + ratio * r + k // rows)
        for r in range(rows)
        for k in range(cols)
    ]
    return lax.ppermute(mine, ("row", "col"), moves)


def gather(mine):
    return lax.all_gather(place(mine), "row", axis=0, tiled=True)


def gather_async(mine):
    rows = lax.axis_size("row")
    here = lax.axis_index("row")
    mine = place(mine)
    parts = [mine]
    for shift in range(1, rows):
        parts.append(lax.ppermute(mine, "row", [(i, i ^ shift) for i in range(rows)]))
    parts = jnp.stack(parts)
    return [lax.dynamic_index_in_dim(parts, here ^ i, 0, keepdims=False) for i in range(rows)]


def contract_gates(gate_flat, weight, ratio):
    parts = weight.reshape(ratio, weight.shape[0] // ratio, weight.shape[1])
    return jnp.stack(
        [
            lax.dot_general(gate_flat, parts[i], NT, preferred_element_type=jnp.float32)
            for i in range(ratio)
        ]
    )


def local(w_rec, w_in, gate_pre, cells, layer_in, h_prev, top_grad):
    layers, row_units, gates, col_units = w_rec.shape
    steps, batch, _ = top_grad.shape
    ratio = row_units // col_units
    rec_w = [w_rec[l].reshape(row_units, gates * col_units) for l in range(layers)]
    in_w = [w_in[l].reshape(row_units, gates * col_units) for l in range(layers)]
    carry = [None] * layers
    store = [None] * layers
    got = None
    bulk = None
    where = {}
    for diagonal in range(steps + layers - 1):
        plan = []
        products = {}
        for layer in range(layers - 1, -1, -1):
            step = steps - 1 - diagonal + (layers - 1 - layer)
            if step < 0 or step >= steps:
                continue
            plan.append(
                {
                    "layer": layer,
                    "step": step,
                    "carry": carry[layer] is not None,
                    "top": layer == layers - 1,
                    "got": layer in where,
                    "at": where.get(layer, 0),
                    "alias": store[layer] is not None,
                    "send": step > 0,
                }
            )
            if step > 0:
                products.setdefault(layer, []).append((len(plan) - 1, rec_w[layer]))
            if layer > 0:
                products.setdefault(layer - 1, []).append((len(plan) - 1, in_w[layer]))
        order = sorted(products, reverse=True)
        partial = run_step(
            plan, [products[l] for l in order], gate_pre, cells, top_grad, got, carry, store
        )
        if partial is not None:
            if bulk is not None:
                partial, bulk = lax.optimization_barrier((partial, bulk))
            mine = jnp.sum(swap(partial), axis=0)
            if steps - 1 - diagonal + layers - 1 == CUT:
                bulk = contract_gates(store[0][CUT * batch :], in_w[0], ratio)
                mine, bulk = lax.optimization_barrier((mine, bulk))
                bulk = swap(bulk)
            got = gather(mine)
            where = {layer: at for at, layer in enumerate(order)}
    rest = contract_gates(store[0][: CUT * batch], in_w[0], ratio)
    saved_rec = h_prev.reshape(layers, steps * batch, row_units)
    saved_in = layer_in.reshape(layers, steps * batch, row_units)
    total = jnp.float32(0.0)
    for l in range(layers):
        gram = lax.dot_general(store[l], store[l], NT, preferred_element_type=jnp.float32)
        gram_h = lax.dot_general(saved_rec[l], saved_rec[l], NT, preferred_element_type=jnp.float32)
        gram_h = gram_h + lax.dot_general(
            saved_in[l], saved_in[l], NT, preferred_element_type=jnp.float32
        )
        total = total + jnp.sum(gram * gram_h)
    devices = lax.axis_size("row") * lax.axis_size("col")
    spread = jnp.broadcast_to(total, (devices, 8, 128))
    spread = lax.all_to_all(spread, ("row", "col"), 0, 0, tiled=True)
    sumsq = jnp.maximum(jnp.sum(spread[:, 0, 0]), 0.0)
    width = row_units * lax.axis_size("row")
    scale = 1.0 / jnp.maximum(jnp.sqrt(sumsq / (8.0 * layers * width * width)), 0.05)
    scale = scale.reshape(1, 1)
    rest, scale = lax.optimization_barrier((rest, scale))
    rest = swap(rest)
    out = ()
    for l in range(layers - 1, -1, -1):
        out = tuple(layer_grads(l, scale, saved_rec, saved_in, store[l], out))
        if l == layers - 1:
            rest, *out = lax.optimization_barrier((rest, *out))
            mine = jnp.concatenate([jnp.sum(bulk, axis=0), jnp.sum(rest, axis=0)])
            parts = gather_async(mine)
    rows = lax.axis_size("row")
    count = (steps - CUT) * batch // rows
    input_grad = jnp.concatenate([p[count:] for p in parts] + [p[:count] for p in parts])
    return (out[0], out[1], input_grad.reshape(steps, batch, col_units))


def solution(mesh):
    placed = (
        P(None, "row", None, "col"),
        P(None, "row", None, "col"),
        P(None, None, None, None, "col"),
        P(None, None, None, "col"),
        P(None, None, None, "row"),
        P(None, None, None, "row"),
        P(None, None, "col"),
    )
    return jax.shard_map(
        local,
        mesh=mesh,
        in_specs=placed,
        out_specs=(P(None, "row", None, "col"), P(None, "row", None, "col"), P(None, None, "col")),
        check_vma=False,
    )
```

profile of v0, /device:TPU:5, one launch (start us, length us, event | category | flops | bytes accessed | tf_op | source)
XLA Modules:
  0.0 360.2 jit_solution(3957826166284669812)
XLA Ops:
  0.6 2.2 slice-done
  2.8 3.6 copy.25
  6.4 1.3 copy-done.3
  7.7 4.1 %fusion.15 = (bf16[1,1024,4,512]{3,2,1,0:T(4,128)(2,1)}, bf16[1,1024,4,512]{3,2,1,0:T(4,128)(2,1)S(1)}) fusion(bf16[2,1024,4,512]{3,2,1,0:T(4,128)(2,1)S(1)} %copy-done.3), kind=kLoop, calls=%fused_computation.36 | loop fusion | bytes 16777216 | tf_op jit(solution)/shard_map/slice | solution.py:241
  11.8 3.4 copy.24
  15.2 6.9 %shard_map.94 = (bf16[384,2048]{1,0:T(8,128)(2,1)}, f32[64,512]{1,0:T(8,128)}, f32[2,128,512]{2,1,0:T(8,128)}) custom-call(f32[2,6,64,4,512]{4,3,2,1,0:T(4,128)} %refs_0_.13, f32[2,7,64,512]{3,2,1,0:T(8,128)} %refs_2_.13, f32[2,7,64,512]{3,2,1,0:T(8,128)} %refs_2_.13, f32[6,64,512]{2,1,0:T(8,128)} %refs_4_.9, bf16[1024,2048]{1,0:T(8,128)(2,1)} %bitcast.102, ...), custom_call_target="tpu_custom_call" | custom-call | flops 536871936 | bytes 9388608 | tf_op jit(solution)/shard_map/pallas_call | solution.py:124
  22.1 19.2 %all_to_all.45 = f32[8,32,512]{2,1,0:T(8,128)S(1)} all-to-all(f32[8,32,512]{2,1,0:T(8,128)} %bitcast.128), channel_id=1, replica_groups=mesh['row'=4,'col'=8] {'col'}, dimensions={0} | all-to-all | bytes 1048576 | tf_op jit(solution)/shard_map/all_to_all | solution.py:197
  41.3 2.4 collective-permute-start
  43.7 5.5 %copy.26 = bf16[128,8,4,512]{3,1,2,0:T(8,128)(2,1)} copy(bf16[128,8,4,512]{3,2,1,0:T(4,128)(2,1)} %bitcast.108) | data formatting | bytes 8388608
  49.3 9.6 %all_gather.18.refs_5_.refs_9_ = f32[128,512]{1,0:T(8,128)} all-gather(f32[32,512]{1,0:T(8,128)S(1)} %collective-permute-done), channel_id=1, replica_groups=mesh['row'=4,'col'=8] {'row'}, dimensions={0}, use_global_device_ids=true | all-gather | bytes 327680 | tf_op jit(solution)/shard_map/all_gather | solution.py:213
  58.8 10.2 %shard_map.95 = (bf16[384,2048]{1,0:T(8,128)(2,1)}, f32[64,512]{1,0:T(8,128)}, bf16[384,2048]{1,0:T(8,128)(2,1)}, f32[64,512]{1,0:T(8,128)}, f32[2,128,512]{2,1,0:T(8,128)}) custom-call(f32[2,6,64,4,512]{4,3,2,1,0:T(4,128)} %refs_0_.13, f32[2,7,64,512]{3,2,1,0:T(8,128)} %refs_2_.13, f32[2,7,64,512]{3,2,1,0:T(8,128)} %refs_2_.13, ...), custom_call_target="tpu_custom_call", output_to_operand_aliasing={{0}: (13, {})} | custom-call | flops 805307392 | bytes 13582912 | tf_op jit(solution)/shard_map/pallas_call | solution.py:124
  69.1 18.2 %all_to_all.46 = f32[8,32,512]{2,1,0:T(8,128)S(1)} all-to-all(f32[8,32,512]{2,1,0:T(8,128)} %bitcast.127), channel_id=1, replica_groups=mesh['row'=4,'col'=8] {'col'}, dimensions={0} | all-to-all | bytes 1048576 | tf_op jit(solution)/shard_map/all_to_all | solution.py:197
  87.3 2.4 collective-permute-start.1
  89.7 4.1 %collective-permute-done.1 = f32[32,512]{1,0:T(8,128)S(1)} collective-permute-done((f32[32,512]{1,0:T(8,128)S(1)}, f32[32,512]{1,0:T(8,128)S(1)}, u32[]{:S(2)}, u32[]{:S(2)}) %collective-permute-start.1) | collective-permute-done | bytes 65568 | tf_op jit(solution)/shard_map/ppermute | solution.py:209
  93.8 9.9 %all_gather.19.refs_5_.refs_10_ = f32[128,512]{1,0:T(8,128)} all-gather(f32[32,512]{1,0:T(8,128)S(1)} %collective-permute-done.1), channel_id=1, replica_groups=mesh['row'=4,'col'=8] {'row'}, dimensions={0}, use_global_device_ids=true | all-gather | bytes 327680 | tf_op jit(solution)/shard_map/all_gather | solution.py:213
  103.7 10.3 %shard_map.96 = (bf16[384,2048]{1,0:T(8,128)(2,1)}, f32[64,512]{1,0:T(8,128)}, bf16[384,2048]{1,0:T(8,128)(2,1)}, f32[64,512]{1,0:T(8,128)}, f32[2,128,512]{2,1,0:T(8,128)}) custom-call(f32[2,6,64,4,512]{4,3,2,1,0:T(4,128)} %refs_0_.13, f32[2,7,64,512]{3,2,1,0:T(8,128)} %refs_2_.13, ...), custom_call_target="tpu_custom_call", output_to_operand_aliasing={{0}: (14, {}), {2}: (15, {})} | custom-call | flops 805307392 | bytes 13582912 | tf_op jit(solution)/shard_map/pallas_call | solution.py:124
  114.0 16.3 %all_to_all.47 = f32[8,32,512]{2,1,0:T(8,128)S(1)} all-to-all(f32[8,32,512]{2,1,0:T(8,128)} %bitcast.125), channel_id=1, replica_groups=mesh['row'=4,'col'=8] {'col'}, dimensions={0} | all-to-all | bytes 1048576 | tf_op jit(solution)/shard_map/all_to_all | solution.py:197
  130.4 2.4 collective-permute-start.2
  132.8 4.1 %collective-permute-done.2 = f32[32,512]{1,0:T(8,128)S(1)} collective-permute-done((f32[32,512]{1,0:T(8,128)S(1)}, f32[32,512]{1,0:T(8,128)S(1)}, u32[]{:S(2)}, u32[]{:S(2)}) %collective-permute-start.2) | collective-permute-done | bytes 65568 | tf_op jit(solution)/shard_map/ppermute | solution.py:209
  136.9 11.1 %all_gather.20.refs_5_.refs_10_ = f32[128,512]{1,0:T(8,128)} all-gather(f32[32,512]{1,0:T(8,128)S(1)} %collective-permute-done.2), channel_id=1, replica_groups=mesh['row'=4,'col'=8] {'row'}, dimensions={0}, use_global_device_ids=true | all-gather | bytes 327680 | tf_op jit(solution)/shard_map/all_gather | solution.py:213
  147.9 10.3 %shard_map.97 = (bf16[384,2048]{1,0:T(8,128)(2,1)}, f32[64,512]{1,0:T(8,128)}, bf16[384,2048]{1,0:T(8,128)(2,1)}, f32[64,512]{1,0:T(8,128)}, f32[2,128,512]{2,1,0:T(8,128)}) custom-call(f32[2,6,64,4,512]{4,3,2,1,0:T(4,128)} %refs_0_.13, f32[2,7,64,512]{3,2,1,0:T(8,128)} %refs_2_.13, ...), custom_call_target="tpu_custom_call", output_to_operand_aliasing={{0}: (14, {}), {2}: (15, {})} | custom-call | flops 805307392 | bytes 13582912 | tf_op jit(solution)/shard_map/pallas_call | solution.py:124
  158.2 16.3 %all_to_all.48 = f32[8,32,512]{2,1,0:T(8,128)S(1)} all-to-all(f32[8,32,512]{2,1,0:T(8,128)} %bitcast.126), channel_id=1, replica_groups=mesh['row'=4,'col'=8] {'col'}, dimensions={0} | all-to-all | bytes 1048576 | tf_op jit(solution)/shard_map/all_to_all | solution.py:197
  174.5 2.4 collective-permute-start.3
  176.9 4.1 %collective-permute-done.3 = f32[32,512]{1,0:T(8,128)S(1)} collective-permute-done((f32[32,512]{1,0:T(8,128)S(1)}, f32[32,512]{1,0:T(8,128)S(1)}, u32[]{:S(2)}, u32[]{:S(2)}) %collective-permute-start.3) | collective-permute-done | bytes 65568 | tf_op jit(solution)/shard_map/ppermute | solution.py:209
  181.1 10.9 %all_gather.21.refs_5_.refs_10_ = f32[128,512]{1,0:T(8,128)} all-gather(f32[32,512]{1,0:T(8,128)S(1)} %collective-permute-done.3), channel_id=1, replica_groups=mesh['row'=4,'col'=8] {'row'}, dimensions={0}, use_global_device_ids=true | all-gather | bytes 327680 | tf_op jit(solution)/shard_map/all_gather | solution.py:213
  191.9 10.2 %shard_map.98 = (bf16[384,2048]{1,0:T(8,128)(2,1)}, f32[64,512]{1,0:T(8,128)}, bf16[384,2048]{1,0:T(8,128)(2,1)}, f32[64,512]{1,0:T(8,128)}, f32[2,128,512]{2,1,0:T(8,128)}) custom-call(f32[2,6,64,4,512]{4,3,2,1,0:T(4,128)} %refs_0_.13, f32[2,7,64,512]{3,2,1,0:T(8,128)} %refs_2_.13, ...), custom_call_target="tpu_custom_call", output_to_operand_aliasing={{0}: (14, {}), {2}: (15, {})} | custom-call | flops 805307392 | bytes 13582912 | tf_op jit(solution)/shard_map/pallas_call | solution.py:124
  202.1 3.4 all-to-all-start.4
  205.6 3.0 fusion.14
  209.9 1.9 copy-done
  211.8 0.7 convolution_bitcast_fusion
  212.6 0.7 convolution_bitcast_fusion.1
  213.3 1.1 pad_maximum_fusion
  214.5 4.2 %all-to-all-done.4 = f32[8,32,512]{2,1,0:T(8,128)S(1)} async-done(((f32[8,32,512]{2,1,0:T(8,128)}), f32[8,32,512]{2,1,0:T(8,128)S(1)}, u32[]{:S(2)}, u32[]{:S(2)}) %all-to-all-start.4) | async-done | bytes 524320 | tf_op jit(solution)/shard_map/all_to_all | solution.py:197
  218.8 4.2 %all-to-all-start.5 = ((f32[8,64,512]{2,1,0:T(8,128)}), f32[8,64,512]{2,1,0:T(8,128)}, u32[]{:S(2)}, u32[]{:S(2)}) async-start(f32[8,64,512]{2,1,0:T(8,128)} %bitcast.7), calls=%async_computation.5 | async-start | bytes 2097152 | tf_op jit(solution)/shard_map/all_to_all | solution.py:197
  223.7 0.7 copy-done.7
  224.5 3.0 collective-permute-start.4
  227.5 1.4 convolution_add_fusion
  228.9 22.8 %collective-permute-done.4 = f32[32,512]{1,0:T(8,128)S(1)} collective-permute-done((f32[32,512]{1,0:T(8,128)S(1)}, f32[32,512]{1,0:T(8,128)S(1)}, u32[]{:S(2)}, u32[]{:S(2)}) %collective-permute-start.4) | collective-permute-done | bytes 65568 | tf_op jit(solution)/shard_map/ppermute | solution.py:209
  251.7 6.7 %all_gather.22.refs_5_.refs_10_ = f32[128,512]{1,0:T(8,128)} all-gather(f32[32,512]{1,0:T(8,128)S(1)} %collective-permute-done.4), channel_id=1, replica_groups=mesh['row'=4,'col'=8] {'row'}, dimensions={0}, use_global_device_ids=true | all-gather | bytes 327680 | tf_op jit(solution)/shard_map/all_gather | solution.py:213
  258.4 8.2 %shard_map.99 = (bf16[384,2048]{1,0:T(8,128)(2,1)}, bf16[384,2048]{1,0:T(8,128)(2,1)}, f32[64,512]{1,0:T(8,128)}, f32[2,64,512]{2,1,0:T(8,128)}) custom-call(f32[2,6,64,4,512]{4,3,2,1,0:T(4,128)} %refs_0_.13, f32[2,7,64,512]{3,2,1,0:T(8,128)} %refs_2_.13, f32[2,7,64,512]{3,2,1,0:T(8,128)} %refs_2_.13, ...), custom_call_target="tpu_custom_call", output_to_operand_aliasing={{0}: (13, {}), {1}: (14, {})} | custom-call | flops 536871936 | bytes 9388608 | tf_op jit(solution)/shard_map/pallas_call | solution.py:124
  266.6 3.4 all-to-all-start.6
  270.6 1.4 convolution_add_fusion.1
  272.0 4.0 %all-to-all-done.6 = f32[8,16,512]{2,1,0:T(8,128)S(1)} async-done(((f32[8,16,512]{2,1,0:T(8,128)}), f32[8,16,512]{2,1,0:T(8,128)S(1)}, u32[]{:S(2)}, u32[]{:S(2)}) %all-to-all-start.6) | async-done | bytes 262176 | tf_op jit(solution)/shard_map/all_to_all | solution.py:197
  276.0 3.5 collective-permute-start.5
  279.6 1.7 fusion.3
  281.2 0.9 collective-permute-done.5
  282.2 10.9 %all_gather.23.refs_4_ = f32[64,512]{1,0:T(8,128)} all-gather(f32[16,512]{1,0:T(8,128)S(1)} %collective-permute-done.5), channel_id=1, replica_groups=mesh['row'=4,'col'=8] {'row'}, dimensions={0}, use_global_device_ids=true | all-gather | bytes 163840 | tf_op jit(solution)/shard_map/all_gather | solution.py:213
  293.1 2.3 shard_map.100.flat_ref
  295.4 2.7 convolution_bitcast_fusion.2
  298.2 1.7 fusion.2
  301.1 0.7 broadcast_in_dim.3
  301.7 3.2 all-to-all-start.7
  305.0 2.4 convolution_bitcast_fusion.3
  307.4 0.8 pad_maximum_fusion.2
  308.2 3.9 %all-to-all-done.7 = f32[32,8,128]{2,1,0:T(8,128)S(1)} async-done(((f32[32,8,128]{2,1,0:T(8,128)}), f32[32,8,128]{2,1,0:T(8,128)S(1)}, u32[]{:S(2)}, u32[]{:S(2)}) %all-to-all-start.7) | async-done | bytes 131104 | tf_op jit(solution)/shard_map/all_to_all | solution.py:298
  313.5 4.0 %all-to-all-start.8 = ((f32[8,32,512]{2,1,0:T(8,128)}), f32[8,32,512]{2,1,0:T(8,128)S(1)}, u32[]{:S(2)}, u32[]{:S(2)}) async-start(f32[8,32,512]{2,1,0:T(8,128)} %bitcast.18), calls=%async_computation.8 | async-start | bytes 1048576 | tf_op jit(solution)/shard_map/all_to_all | solution.py:197
  317.5 1.3 reduce_sum.108
  318.8 11.5 %shard_map.101 = (bf16[2,1024,4,512]{3,2,1,0:T(4,128)(2,1)}, bf16[2,1024,4,512]{3,2,1,0:T(4,128)(2,1)}) custom-call(f32[1,1]{1,0:T(1,128)} %bitcast.15.scale_ref, bf16[2,384,1024]{2,1,0:T(8,128)(2,1)} %bitcast.120, bf16[2,384,1024]{2,1,0:T(8,128)(2,1)} %bitcast.122, bf16[384,2048]{1,0:T(8,128)(2,1)} %get-tuple-element.72.flat_ref), custom_call_target="tpu_custom_call" | custom-call | flops 3221225472 | bytes 8388608 | tf_op jit(solution)/shard_map/pallas_call | solution.py:170
  330.3 1.1 all-to-all-done.8
  331.5 2.0 collective-permute-start.6
  333.5 10.8 %collective-permute-done.6 = f32[96,512]{1,0:T(8,128)S(1)} collective-permute-done((f32[96,512]{1,0:T(8,128)S(1)}, f32[96,512]{1,0:T(8,128)S(1)}, u32[]{:S(2)}, u32[]{:S(2)}) %collective-permute-start.6) | collective-permute-done | bytes 196640 | tf_op jit(solution)/shard_map/ppermute | solution.py:209
  344.4 3.1 collective-permute-start.8
  347.5 11.5 %shard_map.102 = (bf16[2,1024,4,512]{3,2,1,0:T(4,128)(2,1)}, bf16[2,1024,4,512]{3,2,1,0:T(4,128)(2,1)}) custom-call(f32[1,1]{1,0:T(1,128)} %bitcast.15.scale_ref, bf16[2,384,1024]{2,1,0:T(8,128)(2,1)} %bitcast.121, bf16[2,384,1024]{2,1,0:T(8,128)(2,1)} %bitcast.123, ...), custom_call_target="tpu_custom_call", output_to_operand_aliasing={{0}: (4, {}), {1}: (5, {})} | custom-call | flops 3221225472 | bytes 8388608 | tf_op jit(solution)/shard_map/pallas_call | solution.py:170
  359.3 0.9 copy-done.10
  (50 shorter events, 3.9 us)
Async XLA Ops:
  0.6 2.2 slice-start
  2.8 4.9 %copy-start.3 = (bf16[2,1024,4,512]{3,2,1,0:T(4,128)(2,1)S(1)}, bf16[2,1024,4,512]{3,2,1,0:T(4,128)(2,1)}, u32[]{:S(2)}) copy-start(bf16[2,1024,4,512]{3,2,1,0:T(4,128)(2,1)} %param.7) | copy-start | bytes 25165828
  41.3 7.9 %collective-permute-start = (f32[32,512]{1,0:T(8,128)S(1)}, f32[32,512]{1,0:T(8,128)S(1)}, u32[]{:S(2)}, u32[]{:S(2)}) collective-permute-start(f32[32,512]{1,0:T(8,128)S(1)} %reduce_sum.99), channel_id=1, source_target_pairs={{0,0},{1,8},{2,16},{3,24},{4,1},{5,9},{6,17},{7,25},{8,2},{9,10},{... | collective-permute-start | bytes 196616 | tf_op jit(solution)/shard_map/ppermute | solution.py:209
  87.3 6.5 %collective-permute-start.1 = (f32[32,512]{1,0:T(8,128)S(1)}, f32[32,512]{1,0:T(8,128)S(1)}, u32[]{:S(2)}, u32[]{:S(2)}) collective-permute-start(f32[32,512]{1,0:T(8,128)S(1)} %reduce_sum.100), channel_id=1, source_target_pairs={{0,0},{1,8},{2,16},{3,24},{4,1},{5,9},{6,17},{7,25},{8,2},{9,10},{... | collective-permute-start | bytes 196616 | tf_op jit(solution)/shard_map/ppermute | solution.py:209
  130.4 6.5 %collective-permute-start.2 = (f32[32,512]{1,0:T(8,128)S(1)}, f32[32,512]{1,0:T(8,128)S(1)}, u32[]{:S(2)}, u32[]{:S(2)}) collective-permute-start(f32[32,512]{1,0:T(8,128)S(1)} %reduce_sum.101), channel_id=1, source_target_pairs={{0,0},{1,8},{2,16},{3,24},{4,1},{5,9},{6,17},{7,25},{8,2},{9,10},{... | collective-permute-start | bytes 196616 | tf_op jit(solution)/shard_map/ppermute | solution.py:209
  174.5 6.5 %collective-permute-start.3 = (f32[32,512]{1,0:T(8,128)S(1)}, f32[32,512]{1,0:T(8,128)S(1)}, u32[]{:S(2)}, u32[]{:S(2)}) collective-permute-start(f32[32,512]{1,0:T(8,128)S(1)} %reduce_sum.102), channel_id=1, source_target_pairs={{0,0},{1,8},{2,16},{3,24},{4,1},{5,9},{6,17},{7,25},{8,2},{9,10},{... | collective-permute-start | bytes 196616 | tf_op jit(solution)/shard_map/ppermute | solution.py:209
  202.1 16.6 %all-to-all-start.4 = ((f32[8,32,512]{2,1,0:T(8,128)}), f32[8,32,512]{2,1,0:T(8,128)S(1)}, u32[]{:S(2)}, u32[]{:S(2)}) async-start(f32[8,32,512]{2,1,0:T(8,128)} %bitcast.124), calls=%async_computation.4 | async-start | bytes 1048576 | tf_op jit(solution)/shard_map/all_to_all | solution.py:197
  209.2 3.3 copy-start.4
  209.2 2.6 copy-start
  209.9 3.4 copy-start.5
  213.3 9.7 %copy-start.6 = (bf16[2,6,64,1024]{3,2,1,0:T(8,128)(2,1)S(1)}, bf16[2,6,64,1024]{3,2,1,0:T(8,128)(2,1)}, u32[]{:S(2)}) copy-start(bf16[2,6,64,1024]{3,2,1,0:T(8,128)(2,1)} %param.12) | copy-start | bytes 4718596
  218.8 47.8 %all-to-all-start.5 = ((f32[8,64,512]{2,1,0:T(8,128)}), f32[8,64,512]{2,1,0:T(8,128)}, u32[]{:S(2)}, u32[]{:S(2)}) async-start(f32[8,64,512]{2,1,0:T(8,128)} %bitcast.7), calls=%async_computation.5 | async-start | bytes 2097152 | tf_op jit(solution)/shard_map/all_to_all | solution.py:197
  223.0 1.4 copy-start.7
  224.5 27.2 %collective-permute-start.4 = (f32[32,512]{1,0:T(8,128)S(1)}, f32[32,512]{1,0:T(8,128)S(1)}, u32[]{:S(2)}, u32[]{:S(2)}) collective-permute-start(f32[32,512]{1,0:T(8,128)S(1)} %reduce_sum.103), channel_id=1, source_target_pairs={{0,0},{1,8},{2,16},{3,24},{4,1},{5,9},{6,17},{7,25},{8,2},{9,10},{... | collective-permute-start | bytes 196616 | tf_op jit(solution)/shard_map/ppermute | solution.py:209
  266.6 9.4 %all-to-all-start.6 = ((f32[8,16,512]{2,1,0:T(8,128)}), f32[8,16,512]{2,1,0:T(8,128)S(1)}, u32[]{:S(2)}, u32[]{:S(2)}) async-start(f32[8,16,512]{2,1,0:T(8,128)} %bitcast.129), calls=%async_computation.6 | async-start | bytes 524288 | tf_op jit(solution)/shard_map/all_to_all | solution.py:197
  270.0 9.5 %copy-start.2 = (bf16[384,2048]{1,0:T(8,128)(2,1)S(1)}, bf16[384,2048]{1,0:T(8,128)(2,1)}, u32[]{:S(2)}) copy-start(bf16[384,2048]{1,0:T(8,128)(2,1)} %get-tuple-element.72.flat_ref) | copy-start | bytes 4718596
  270.6 9.0 %copy-start.8 = (f32[384,384]{1,0:T(8,128)S(1)}, f32[384,384]{1,0:T(8,128)}, u32[]{:S(2)}) copy-start(f32[384,384]{1,0:T(8,128)} %convolution_add_fusion) | copy-start | bytes 1769476
  276.0 6.1 %collective-permute-start.5 = (f32[16,512]{1,0:T(8,128)S(1)}, f32[16,512]{1,0:T(8,128)S(1)}, u32[]{:S(2)}, u32[]{:S(2)}) collective-permute-start(f32[16,512]{1,0:T(8,128)S(1)} %reduce_sum.104), channel_id=1, source_target_pairs={{0,0},{1,8},{2,16},{3,24},{4,1},{5,9},{6,17},{7,25},{8,2},{9,10},{... | collective-permute-start | bytes 98312 | tf_op jit(solution)/shard_map/ppermute | solution.py:209
  295.4 2.7 copy-start.1
  295.4 2.8 copy-start.9
  301.7 10.4 %all-to-all-start.7 = ((f32[32,8,128]{2,1,0:T(8,128)}), f32[32,8,128]{2,1,0:T(8,128)S(1)}, u32[]{:S(2)}, u32[]{:S(2)}) async-start(f32[32,8,128]{2,1,0:T(8,128)} %broadcast_in_dim.3), calls=%async_computation.7 | async-start | bytes 262144 | tf_op jit(solution)/shard_map/all_to_all | solution.py:298
  313.5 17.9 %all-to-all-start.8 = ((f32[8,32,512]{2,1,0:T(8,128)}), f32[8,32,512]{2,1,0:T(8,128)S(1)}, u32[]{:S(2)}, u32[]{:S(2)}) async-start(f32[8,32,512]{2,1,0:T(8,128)} %bitcast.18), calls=%async_computation.8 | async-start | bytes 1048576 | tf_op jit(solution)/shard_map/all_to_all | solution.py:197
  331.5 12.8 %collective-permute-start.6 = (f32[96,512]{1,0:T(8,128)S(1)}, f32[96,512]{1,0:T(8,128)S(1)}, u32[]{:S(2)}, u32[]{:S(2)}) collective-permute-start(f32[96,512]{1,0:T(8,128)S(1)} %pad_maximum_fusion.3), channel_id=1, source_target_pairs={{0,0},{1,8},{2,16},{3,24},{4,1},{5,9},{6,17},{7,25},{8,2},{9,10},{... | collective-permute-start | bytes 589832 | tf_op jit(solution)/shard_map/ppermute | solution.py:209
  344.3 14.7 %collective-permute-start.9 = (f32[96,512]{1,0:T(8,128)S(1)}, f32[96,512]{1,0:T(8,128)S(1)}, u32[]{:S(2)}, u32[]{:S(2)}) collective-permute-start(f32[96,512]{1,0:T(8,128)S(1)} %collective-permute-done.6), channel_id=1, source_target_pairs={{0,24},{8,16},{16,8},{24,0},{1,25},{9,17},{17,9},{25,1},{2,26},{10... | collective-permute-start | bytes 589832 | tf_op jit(solution)/shard_map/ppermute | solution.py:222
  344.4 14.6 %collective-permute-start.8 = (f32[96,512]{1,0:T(8,128)S(1)}, f32[96,512]{1,0:T(8,128)S(1)}, u32[]{:S(2)}, u32[]{:S(2)}) collective-permute-start(f32[96,512]{1,0:T(8,128)S(1)} %collective-permute-done.6), channel_id=1, source_target_pairs={{0,16},{8,24},{16,0},{24,8},{1,17},{9,25},{17,1},{25,9},{2,18},{10... | collective-permute-start | bytes 589832 | tf_op jit(solution)/shard_map/ppermute | solution.py:222
  347.5 11.5 %collective-permute-start.7 = (f32[96,512]{1,0:T(8,128)S(1)}, f32[96,512]{1,0:T(8,128)S(1)}, u32[]{:S(2)}, u32[]{:S(2)}) collective-permute-start(f32[96,512]{1,0:T(8,128)S(1)} %collective-permute-done.6), channel_id=1, source_target_pairs={{0,8},{8,0},{16,24},{24,16},{1,9},{9,1},{17,25},{25,17},{2,10},{10... | collective-permute-start | bytes 589832 | tf_op jit(solution)/shard_map/ppermute | solution.py:222
  359.3 0.9 copy-start.10
where the time goes:
time: 362 us; the launch traced here: 360 us
  blocking collectives  129 us (36%)
  Pallas kernels  81.4 us (22%)
  waiting for transfers between devices  60.2 us (17%)
  starting transfers between devices  39.5 us (11%)
  local copies, waits for them, and re-layouts  28.9 us (8%)
  matrix products  14 us (4%)
  other arithmetic  4.22 us (1%)
    all_to_all x4, blocking collectives, swap(): return lax.all_to_all(pieces, 'col', 0, 0, tiled=True)  70 us
    all_gather x6, blocking collectives, gather(): return lax.all_gather(place(mine), 'row', axis=0, tiled=True)  59 us
    pallas_call x7, Pallas kernels, run_step(): pl.pallas_call(functools.partial(step_kernel, plan, [[which for which, _...  58.4 us
    ppermute x7, waiting for transfers between devices, place(): return lax.ppermute(mine, ('row', 'col'), moves)  46.9 us
    pallas_call x2, Pallas kernels, layer_grads(): pl.pallas_call(grads_kernel_keep if before else grads_kernel, grid=(rows...  23 us
    unnamed x34, local copies, waits for them, and re-layouts  18.7 us
    ppermute x7, starting transfers between devices, place(): return lax.ppermute(mine, ('row', 'col'), moves)  18 us
    all_to_all x4, starting transfers between devices, swap(): return lax.all_to_all(pieces, 'col', 0, 0, tiled=True)  15 us
  transfers between devices with their start and end apart: 15, of which 10 were waited for; matrix products, arithmetic and copies ran while one was open for 6% of the time, Pallas kernels for 9%

commit v1 on v0

--- a/solution.py
+++ b/solution.py
@@ -13,12 +13,14 @@
 CUT = 2
 
 
-def step_kernel(plan, products, *refs):
+def step_kernel(plan, products, parts, *refs):
     refs = list(refs)
     live = []
     for entry in plan:
-        need = ["gate", "prev", "now"] + [name for name in ("carry", "top", "got") if entry[name]]
+        need = ["gate", "prev", "now"] + [name for name in ("carry", "top") if entry[name]]
         live.append({name: refs.pop(0) for name in need})
+    pieces = [refs.pop(0) for _ in range(parts)]
+    here = refs.pop(0) if parts else None
     weights = [[refs.pop(0) for _ in terms] for terms in products]
     for entry in plan:
         if entry["alias"]:
@@ -30,8 +32,15 @@
             out["carry"] = refs.pop(0)
         outs.append(out)
 
+    partial = refs.pop(0) if products else None
+    whole = refs.pop(0) if parts else None
+
     @pl.when(pl.program_id(0) == 0)
     def _():
+        for s, piece in enumerate(pieces):
+            owner = lax.rem(here[0, 0] + parts - s, parts)
+            size = piece.shape[0]
+            whole[pl.ds(pl.multiple_of(owner * size, size), size), :] = piece[...]
         for entry, ins, out in zip(plan, live, outs):
             units = ins["prev"].shape[-1]
             gate = ins["gate"]
@@ -45,24 +54,23 @@
                 hid_grad = ins["top"][0]
             if entry["got"]:
                 batch = out["grads"].shape[0]
-                got = ins["got"][pl.ds(entry["at"] * batch, batch), :]
+                got = whole[pl.ds(entry["at"] * batch, batch), :]
                 hid_grad = got if hid_grad is None else hid_grad + got
             cell_grad = hid_grad * out_gate * (1.0 - tanh_cell * tanh_cell)
             if entry["carry"]:
                 cell_grad = cell_grad + ins["carry"][...]
-            parts = (
+            quads = (
                 cell_grad * cand_gate * in_gate * (1.0 - in_gate),
                 cell_grad * ins["prev"][0, 0] * forget * (1.0 - forget),
                 cell_grad * in_gate * (1.0 - cand_gate * cand_gate),
                 hid_grad * tanh_cell * out_gate * (1.0 - out_gate),
             )
-            for k, part in enumerate(parts):
+            for k, part in enumerate(quads):
                 out["grads"][:, k * units : (k + 1) * units] = part.astype(jnp.bfloat16)
             if entry["send"]:
                 out["carry"][...] = cell_grad * forget
 
     if products:
-        partial = refs.pop(0)
         for slot, (terms, w_refs) in enumerate(zip(products, weights)):
             total = None
             for which, w_ref in zip(terms, w_refs):
@@ -93,8 +101,13 @@
             take(carry[l], (batch, units), (0, 0))
         if entry["top"]:
             take(top_grad, (1, batch, units), (t, 0, 0))
-        if entry["got"]:
-            take(got, got.shape, (0, 0))
+    scratch = []
+    if got is not None:
+        for piece in got:
+            take(piece, piece.shape, (0, 0))
+        ins.append(lax.axis_index("row").astype(jnp.int32).reshape(1, 1))
+        in_specs.append(pl.BlockSpec(memory_space=pltpu.SMEM))
+        scratch.append(pltpu.VMEM((len(got) * got[0].shape[0], units), jnp.float32))
     rows = None
     for terms in products:
         for _, weight in terms:
@@ -122,11 +135,17 @@
         out_specs.append(pl.BlockSpec((1, count, tile), lambda i: (i // per, 0, i % per)))
         flops = sum(len(terms) for terms in products) * 2 * batch * rows * 4 * units
     outs = pl.pallas_call(
-        functools.partial(step_kernel, plan, [[which for which, _ in terms] for terms in products]),
+        functools.partial(
+            step_kernel,
+            plan,
+            [[which for which, _ in terms] for terms in products],
+            len(got) if got is not None else 0,
+        ),
         grid=(grid,),
         out_shape=out_shape,
         in_specs=in_specs,
         out_specs=out_specs,
+        scratch_shapes=scratch,
         input_output_aliases=aliases,
         compiler_params=pltpu.CompilerParams(vmem_limit_bytes=VMEM_LIMIT),
         cost_estimate=pl.CostEstimate(
@@ -163,7 +182,7 @@
 def layer_grads(layer, scale, saved_rec, saved_in, flat, before):
     layers, count, rows = saved_rec.shape
     units = flat.shape[1] // 4
-    tile = min(256, rows)
+    tile = min(128, rows)
     block = pl.BlockSpec((1, count, tile), lambda j: (layer, 0, j))
     kept = pl.BlockSpec(memory_space=pl.ANY)
     out = pl.BlockSpec((1, tile, 4, units), lambda j: (layer, j, 0, 0))
@@ -210,18 +229,31 @@
 
 
 def gather(mine):
-    return lax.all_gather(place(mine), "row", axis=0, tiled=True)
-
-
-def gather_async(mine):
     rows = lax.axis_size("row")
+    mine = place(mine)
+    return [mine] + [
+        lax.ppermute(mine, "row", [(i, (i + s) % rows) for i in range(rows)])
+        for s in range(1, rows)
+    ]
+
+
+def gather_direct(mine):
+    rows = lax.axis_size("row")
+    cols = lax.axis_size("col")
+    ratio = cols // rows
     here = lax.axis_index("row")
-    mine = place(mine)
-    parts = [mine]
-    for shift in range(1, rows):
-        parts.append(lax.ppermute(mine, "row", [(i, i ^ shift) for i in range(rows)]))
+    parts = []
+    for s in range(rows):
+        moves = [
+            (r * cols + k, (k + s) % rows * cols + ratio * r + k // rows)
+            for r in range(rows)
+            for k in range(cols)
+        ]
+        parts.append(lax.ppermute(mine, ("row", "col"), moves))
     parts = jnp.stack(parts)
-    return [lax.dynamic_index_in_dim(parts, here ^ i, 0, keepdims=False) for i in range(rows)]
+    return [
+        lax.dynamic_index_in_dim(parts, (here - i) % rows, 0, keepdims=False) for i in range(rows)
+    ]
 
 
 def contract_gates(gate_flat, weight, ratio):
@@ -238,8 +270,9 @@
     layers, row_units, gates, col_units = w_rec.shape
     steps, batch, _ = top_grad.shape
     ratio = row_units // col_units
-    rec_w = [w_rec[l].reshape(row_units, gates * col_units) for l in range(layers)]
-    in_w = [w_in[l].reshape(row_units, gates * col_units) for l in range(layers)]
+    flat = (row_units, gates * col_units)
+    rec_w = [None] * (layers - 1) + [w_rec[layers - 1].reshape(flat)]
+    in_w = [None] * (layers - 1) + [w_in[layers - 1].reshape(flat)]
     carry = [None] * layers
     store = [None] * layers
     got = None
@@ -275,7 +308,16 @@
         if partial is not None:
             if bulk is not None:
                 partial, bulk = lax.optimization_barrier((partial, bulk))
-            mine = jnp.sum(swap(partial), axis=0)
+            late = rec_w if diagonal % 2 == 0 else in_w
+            below = layers - 2 - diagonal // 2
+            if below >= 0:
+                source = w_rec if diagonal % 2 == 0 else w_in
+                source, partial = lax.optimization_barrier((source, partial))
+                late[below] = source[below].reshape(flat)
+            partial = swap(partial)
+            if below >= 0:
+                partial, late[below] = lax.optimization_barrier((partial, late[below]))
+            mine = jnp.sum(partial, axis=0)
             if steps - 1 - diagonal + layers - 1 == CUT:
                 bulk = contract_gates(store[0][CUT * batch :], in_w[0], ratio)
                 mine, bulk = lax.optimization_barrier((mine, bulk))
@@ -308,7 +350,7 @@
         if l == layers - 1:
             rest, *out = lax.optimization_barrier((rest, *out))
             mine = jnp.concatenate([jnp.sum(bulk, axis=0), jnp.sum(rest, axis=0)])
-            parts = gather_async(mine)
+            parts = gather_direct(mine)
     rows = lax.axis_size("row")
     count = (steps - CUT) * batch // rows
     input_grad = jnp.concatenate([p[count:] for p in parts] + [p[:count] for p in parts])

time: 362 us -> 360 us (level)
  blocking collectives: 129 us -> 31.8 us
  starting transfers between devices: 39.5 us -> 88.1 us
  waiting for transfers between devices: 60.2 us -> 101 us
  matrix products: 14 us -> 19.5 us
    all_gather x6 -> x0, blocking collectives: 59 us -> none  [gather(): return lax.all_gather(place(mine), 'row', axis=0, tiled=True)]
    ppermute x3 -> x22, starting transfers between devices: 3.21 us -> 45.7 us  [the longest x18 34 us: gather(): lax.ppermute(mine, 'row', [(i, (i + s) % rows) for i in range(rows)])]
    all_to_all x4 -> x2, blocking collectives: 70 us -> 31.8 us  [swap(): return lax.all_to_all(pieces, 'col', 0, 0, tiled=True)]
    ppermute x3 -> x22, waiting for transfers between devices: 0.01 us -> 27.9 us  [the longest x4 15.6 us: gather_direct(): parts.append(lax.ppermute(mine, ('row', 'col'), moves))]
    all_to_all x4 -> x6, waiting for transfers between devices: 9.36 us -> 23.3 us  [swap(): return lax.all_to_all(pieces, 'col', 0, 0, tiled=True)]
    all_to_all x4 -> x6, starting transfers between devices: 15 us -> 25.9 us  [swap(): return lax.all_to_all(pieces, 'col', 0, 0, tiled=True)]
    ppermute x7 -> x6, starting transfers between devices: 18 us -> 12.7 us  [place(): return lax.ppermute(mine, ('row', 'col'), moves)]
    dot_general x4, matrix products: 6.63 us -> 10.3 us  [contract_gates(): lax.dot_general(gate_flat, parts[i], NT, preferred_element_type=jnp.float32)]
  transfers between devices with their start and end apart: 15 -> 35, of which waited for: 10 -> 24; matrix products, arithmetic and copies ran while one was open for 6% -> 7% of each run, Pallas kernels for 9% -> 9%
where the time goes in v1:
time: 360 us; the launch traced here: 358 us
  waiting for transfers between devices  101 us (28%)
  starting transfers between devices  88.1 us (24%)
  Pallas kernels  81.5 us (23%)
  blocking collectives  31.8 us (9%)
  local copies, waits for them, and re-layouts  27.9 us (8%)
  matrix products  19.5 us (5%)
  other arithmetic  5.17 us (1%)
    pallas_call x7, Pallas kernels, run_step(): pl.pallas_call(functools.partial(step_kernel, plan, [[which for which, _...  57.2 us
    ppermute x6, waiting for transfers between devices, place(): return lax.ppermute(mine, ('row', 'col'), moves)  46.1 us
    ppermute x18, starting transfers between devices, gather(): lax.ppermute(mine, 'row', [(i, (i + s) % rows) for i in range(rows)])  34 us
    all_to_all x2, blocking collectives, swap(): return lax.all_to_all(pieces, 'col', 0, 0, tiled=True)  31.8 us
    all_to_all x6, starting transfers between devices, swap(): return lax.all_to_all(pieces, 'col', 0, 0, tiled=True)  25.9 us
    pallas_call x2, Pallas kernels, layer_grads(): pl.pallas_call(grads_kernel_keep if before else grads_kernel, grid=(rows...  24.3 us
    all_to_all x6, waiting for transfers between devices, swap(): return lax.all_to_all(pieces, 'col', 0, 0, tiled=True)  23.3 us
    unnamed x75, local copies, waits for them, and re-layouts  18.2 us
  transfers between devices with their start and end apart: 35, of which 24 were waited for; matrix products, arithmetic and copies ran while one was open for 7% of the time, Pallas kernels for 9%

profile of v1, /device:TPU:5, one launch (start us, length us, event | category | flops | bytes accessed | tf_op | source)
XLA Modules:
  0.0 358.3 jit_solution(3880803312786147050)
XLA Ops:
  0.6 2.2 slice-done
  2.8 3.4 copy.24
  6.2 2.2 slice-done.2
  8.4 3.4 copy.25
  11.8 6.9 %shard_map.94 = (bf16[384,2048]{1,0:T(8,128)(2,1)}, f32[64,512]{1,0:T(8,128)}, f32[2,128,512]{2,1,0:T(8,128)}) custom-call(f32[2,6,64,4,512]{4,3,2,1,0:T(4,128)} %refs_0_.13, f32[2,7,64,512]{3,2,1,0:T(8,128)} %refs_2_.13, f32[2,7,64,512]{3,2,1,0:T(8,128)} %refs_2_.13, f32[6,64,512]{2,1,0:T(8,128)} %refs_4_.9, bf16[1024,2048]{1,0:T(8,128)(2,1)} %bitcast.96, ...), custom_call_target="tpu_custom_call" | custom-call | flops 536871936 | bytes 9388608 | tf_op jit(solution)/shard_map/pallas_call | solution.py:137
  18.7 5.8 %all-to-all-start = ((f32[8,32,512]{2,1,0:T(8,128)}), f32[8,32,512]{2,1,0:T(8,128)S(1)}, u32[]{:S(2)}, u32[]{:S(2)}) async-start(f32[8,32,512]{2,1,0:T(8,128)} %bitcast.121), calls=%async_computation | async-start | bytes 1048576 | tf_op jit(solution)/shard_map/all_to_all | solution.py:216
  24.4 2.2 slice-done.1
  26.6 3.4 copy.26
  30.0 8.2 %all-to-all-done = f32[8,32,512]{2,1,0:T(8,128)S(1)} async-done(((f32[8,32,512]{2,1,0:T(8,128)}), f32[8,32,512]{2,1,0:T(8,128)S(1)}, u32[]{:S(2)}, u32[]{:S(2)}) %all-to-all-start) | async-done | bytes 524320 | tf_op jit(solution)/shard_map/all_to_all | solution.py:216
  40.2 4.7 %collective-permute-done.refs_8_ = f32[32,512]{1,0:T(8,128)S(1)} collective-permute-done((f32[32,512]{1,0:T(8,128)S(1)}, f32[32,512]{1,0:T(8,128)S(1)}, u32[]{:S(2)}, u32[]{:S(2)}) %collective-permute-start) | collective-permute-done | bytes 65568 | tf_op jit(solution)/shard_map/ppermute | solution.py:228
  44.9 2.7 collective-permute-start.3
  47.6 3.1 collective-permute-start.2
  50.7 2.4 collective-permute-done.3.refs_11_
  53.9 9.9 %shard_map.95 = (bf16[384,2048]{1,0:T(8,128)(2,1)}, f32[64,512]{1,0:T(8,128)}, bf16[384,2048]{1,0:T(8,128)(2,1)}, f32[64,512]{1,0:T(8,128)}, f32[2,128,512]{2,1,0:T(8,128)}) custom-call(f32[2,6,64,4,512]{4,3,2,1,0:T(4,128)} %refs_0_.13, f32[2,7,64,512]{3,2,1,0:T(8,128)} %refs_2_.13, f32[2,7,64,512]{3,2,1,0:T(8,128)} %refs_2_.13, ...), custom_call_target="tpu_custom_call", output_to_operand_aliasing={{0}: (16, {})} | custom-call | flops 805307392 | bytes 13582912 | tf_op jit(solution)/shard_map/pallas_call | solution.py:137
  63.8 3.5 all-to-all-start.1
  67.3 2.2 slice-done.3
  69.5 3.3 copy.27
  72.8 6.5 %all-to-all-done.1 = f32[8,32,512]{2,1,0:T(8,128)S(1)} async-done(((f32[8,32,512]{2,1,0:T(8,128)}), f32[8,32,512]{2,1,0:T(8,128)S(1)}, u32[]{:S(2)}, u32[]{:S(2)}) %all-to-all-start.1) | async-done | bytes 524320 | tf_op jit(solution)/shard_map/all_to_all | solution.py:216
  81.3 4.9 %collective-permute-done.4.refs_9_ = f32[32,512]{1,0:T(8,128)S(1)} collective-permute-done((f32[32,512]{1,0:T(8,128)S(1)}, f32[32,512]{1,0:T(8,128)S(1)}, u32[]{:S(2)}, u32[]{:S(2)}) %collective-permute-start.4) | collective-permute-done | bytes 65568 | tf_op jit(solution)/shard_map/ppermute | solution.py:228
  86.2 3.5 collective-permute-start.7
  89.7 2.9 collective-permute-start.6
  92.6 2.4 collective-permute-done.7.refs_12_
  95.8 10.0 %shard_map.96 = (bf16[384,2048]{1,0:T(8,128)(2,1)}, f32[64,512]{1,0:T(8,128)}, bf16[384,2048]{1,0:T(8,128)(2,1)}, f32[64,512]{1,0:T(8,128)}, f32[2,128,512]{2,1,0:T(8,128)}) custom-call(f32[2,6,64,4,512]{4,3,2,1,0:T(4,128)} %refs_0_.13, f32[2,7,64,512]{3,2,1,0:T(8,128)} %refs_2_.13, ...), custom_call_target="tpu_custom_call", output_to_operand_aliasing={{0}: (17, {}), {2}: (18, {})} | custom-call | flops 805307392 | bytes 13582912 | tf_op jit(solution)/shard_map/pallas_call | solution.py:137
  105.8 15.9 %all_to_all.45 = f32[8,32,512]{2,1,0:T(8,128)S(1)} all-to-all(f32[8,32,512]{2,1,0:T(8,128)} %bitcast.119), channel_id=1, replica_groups=mesh['row'=4,'col'=8] {'col'}, dimensions={0} | all-to-all | bytes 1048576 | tf_op jit(solution)/shard_map/all_to_all | solution.py:216
  123.7 4.7 %collective-permute-done.8.refs_9_ = f32[32,512]{1,0:T(8,128)S(1)} collective-permute-done((f32[32,512]{1,0:T(8,128)S(1)}, f32[32,512]{1,0:T(8,128)S(1)}, u32[]{:S(2)}, u32[]{:S(2)}) %collective-permute-start.8) | collective-permute-done | bytes 65568 | tf_op jit(solution)/shard_map/ppermute | solution.py:228
  128.3 3.6 %collective-permute-start.11 = (f32[32,512]{1,0:T(8,128)S(1)}, f32[32,512]{1,0:T(8,128)S(1)}, u32[]{:S(2)}, u32[]{:S(2)}) collective-permute-start(f32[32,512]{1,0:T(8,128)S(1)} %collective-permute-done.8.refs_9_), channel_id=1, source_target_pairs={{0,24},{8,0},{16,8},{24,16},{1,25},{9,1},{17,9},{25,17},{2,26},{10... | collective-permute-start | bytes 196616 | tf_op jit(solution)/shard_map/ppermute | solution.py:235
  132.0 2.7 collective-permute-start.10
  134.6 2.4 collective-permute-done.11.refs_12_
  137.8 10.0 %shard_map.97 = (bf16[384,2048]{1,0:T(8,128)(2,1)}, f32[64,512]{1,0:T(8,128)}, bf16[384,2048]{1,0:T(8,128)(2,1)}, f32[64,512]{1,0:T(8,128)}, f32[2,128,512]{2,1,0:T(8,128)}) custom-call(f32[2,6,64,4,512]{4,3,2,1,0:T(4,128)} %refs_0_.13, f32[2,7,64,512]{3,2,1,0:T(8,128)} %refs_2_.13, ...), custom_call_target="tpu_custom_call", output_to_operand_aliasing={{0}: (17, {}), {2}: (18, {})} | custom-call | flops 805307392 | bytes 13582912 | tf_op jit(solution)/shard_map/pallas_call | solution.py:137
  147.8 15.9 %all_to_all.46 = f32[8,32,512]{2,1,0:T(8,128)S(1)} all-to-all(f32[8,32,512]{2,1,0:T(8,128)} %bitcast.120), channel_id=1, replica_groups=mesh['row'=4,'col'=8] {'col'}, dimensions={0} | all-to-all | bytes 1048576 | tf_op jit(solution)/shard_map/all_to_all | solution.py:216
  165.7 4.7 %collective-permute-done.12.refs_9_ = f32[32,512]{1,0:T(8,128)S(1)} collective-permute-done((f32[32,512]{1,0:T(8,128)S(1)}, f32[32,512]{1,0:T(8,128)S(1)}, u32[]{:S(2)}, u32[]{:S(2)}) %collective-permute-start.12) | collective-permute-done | bytes 65568 | tf_op jit(solution)/shard_map/ppermute | solution.py:228
  170.3 3.6 %collective-permute-start.15 = (f32[32,512]{1,0:T(8,128)S(1)}, f32[32,512]{1,0:T(8,128)S(1)}, u32[]{:S(2)}, u32[]{:S(2)}) collective-permute-start(f32[32,512]{1,0:T(8,128)S(1)} %collective-permute-done.12.refs_9_), channel_id=1, source_target_pairs={{0,24},{8,0},{16,8},{24,16},{1,25},{9,1},{17,9},{25,17},{2,26},{10... | collective-permute-start | bytes 196616 | tf_op jit(solution)/shard_map/ppermute | solution.py:235
  174.0 2.7 collective-permute-start.14
  176.6 2.4 collective-permute-done.15.refs_12_
  179.9 10.0 %shard_map.98 = (bf16[384,2048]{1,0:T(8,128)(2,1)}, f32[64,512]{1,0:T(8,128)}, bf16[384,2048]{1,0:T(8,128)(2,1)}, f32[64,512]{1,0:T(8,128)}, f32[2,128,512]{2,1,0:T(8,128)}) custom-call(f32[2,6,64,4,512]{4,3,2,1,0:T(4,128)} %refs_0_.13, f32[2,7,64,512]{3,2,1,0:T(8,128)} %refs_2_.13, ...), custom_call_target="tpu_custom_call", output_to_operand_aliasing={{0}: (17, {}), {2}: (18, {})} | custom-call | flops 805307392 | bytes 13582912 | tf_op jit(solution)/shard_map/pallas_call | solution.py:137
  189.8 4.1 %all-to-all-start.4 = ((f32[8,32,512]{2,1,0:T(8,128)}), f32[8,32,512]{2,1,0:T(8,128)}, u32[]{:S(2)}, u32[]{:S(2)}) async-start(f32[8,32,512]{2,1,0:T(8,128)} %bitcast.117), calls=%async_computation.4 | async-start | bytes 1048576 | tf_op jit(solution)/shard_map/all_to_all | solution.py:216
  194.0 2.8 fusion.11
  196.7 2.3 fusion.8
  200.1 5.3 %all-to-all-done.4 = f32[8,32,512]{2,1,0:T(8,128)} async-done(((f32[8,32,512]{2,1,0:T(8,128)}), f32[8,32,512]{2,1,0:T(8,128)}, u32[]{:S(2)}, u32[]{:S(2)}) %all-to-all-start.4) | async-done | bytes 524320 | tf_op jit(solution)/shard_map/all_to_all | solution.py:216
  206.5 4.2 %all-to-all-start.5 = ((f32[8,64,512]{2,1,0:T(8,128)}), f32[8,64,512]{2,1,0:T(8,128)}, u32[]{:S(2)}, u32[]{:S(2)}) async-start(f32[8,64,512]{2,1,0:T(8,128)} %bitcast.8), calls=%async_computation.5 | async-start | bytes 2097152 | tf_op jit(solution)/shard_map/all_to_all | solution.py:216
  210.9 2.2 collective-permute-start.16
  213.3 25.3 %collective-permute-done.16.refs_9_ = f32[32,512]{1,0:T(8,128)S(1)} collective-permute-done((f32[32,512]{1,0:T(8,128)S(1)}, f32[32,512]{1,0:T(8,128)S(1)}, u32[]{:S(2)}, u32[]{:S(2)}) %collective-permute-start.16) | collective-permute-done | bytes 65568 | tf_op jit(solution)/shard_map/ppermute | solution.py:228
  244.0 8.0 %shard_map.99 = (bf16[384,2048]{1,0:T(8,128)(2,1)}, bf16[384,2048]{1,0:T(8,128)(2,1)}, f32[64,512]{1,0:T(8,128)}, f32[2,64,512]{2,1,0:T(8,128)}) custom-call(f32[2,6,64,4,512]{4,3,2,1,0:T(4,128)} %refs_0_.13, f32[2,7,64,512]{3,2,1,0:T(8,128)} %refs_2_.13, f32[2,7,64,512]{3,2,1,0:T(8,128)} %refs_2_.13, ...), custom_call_target="tpu_custom_call", output_to_operand_aliasing={{0}: (16, {}), {1}: (17, {})} | custom-call | flops 536871936 | bytes 9388608 | tf_op jit(solution)/shard_map/pallas_call | solution.py:137
  252.0 4.3 %all-to-all-start.6 = ((f32[8,16,512]{2,1,0:T(8,128)}), f32[8,16,512]{2,1,0:T(8,128)S(1)}, u32[]{:S(2)}, u32[]{:S(2)}) async-start(f32[8,16,512]{2,1,0:T(8,128)} %bitcast.122), calls=%async_computation.6 | async-start | bytes 524288 | tf_op jit(solution)/shard_map/all_to_all | solution.py:216
  259.2 2.8 all-to-all-done.6
  262.1 2.8 collective-permute-start.20
  264.9 2.5 convolution_add_fusion.1
  267.3 1.9 collective-permute-done.20.refs_4_
  269.3 4.5 %collective-permute-start.23 = (f32[16,512]{1,0:T(8,128)S(1)}, f32[16,512]{1,0:T(8,128)S(1)}, u32[]{:S(2)}, u32[]{:S(2)}) collective-permute-start(f32[16,512]{1,0:T(8,128)S(1)} %collective-permute-done.20.refs_4_), channel_id=1, source_target_pairs={{0,24},{8,0},{16,8},{24,16},{1,25},{9,1},{17,9},{25,17},{2,26},{10... | collective-permute-start | bytes 98312 | tf_op jit(solution)/shard_map/ppermute | solution.py:235
  273.8 2.3 collective-permute-start.22
  278.6 2.5 shard_map.100.flat_ref
  281.0 2.7 fusion.17
  287.4 3.7 %all-to-all-start.7 = ((f32[32,8,128]{2,1,0:T(8,128)}), f32[32,8,128]{2,1,0:T(8,128)S(1)}, u32[]{:S(2)}, u32[]{:S(2)}) async-start(f32[32,8,128]{2,1,0:T(8,128)} %broadcast_in_dim.3), calls=%async_computation.7 | async-start | bytes 262144 | tf_op jit(solution)/shard_map/all_to_all | solution.py:340
  291.1 2.4 fusion.14
  294.4 3.9 %all-to-all-done.7 = f32[32,8,128]{2,1,0:T(8,128)S(1)} async-done(((f32[32,8,128]{2,1,0:T(8,128)}), f32[32,8,128]{2,1,0:T(8,128)S(1)}, u32[]{:S(2)}, u32[]{:S(2)}) %all-to-all-start.7) | async-done | bytes 131104 | tf_op jit(solution)/shard_map/all_to_all | solution.py:340
  299.7 4.0 %all-to-all-start.8 = ((f32[8,32,512]{2,1,0:T(8,128)}), f32[8,32,512]{2,1,0:T(8,128)S(1)}, u32[]{:S(2)}, u32[]{:S(2)}) async-start(f32[8,32,512]{2,1,0:T(8,128)} %bitcast.19), calls=%async_computation.8 | async-start | bytes 1048576 | tf_op jit(solution)/shard_map/all_to_all | solution.py:216
  305.0 12.2 %shard_map.101 = (bf16[2,1024,4,512]{3,2,1,0:T(4,128)(2,1)}, bf16[2,1024,4,512]{3,2,1,0:T(4,128)(2,1)}) custom-call(f32[1,1]{1,0:T(1,128)} %bitcast.16.scale_ref, bf16[2,384,1024]{2,1,0:T(8,128)(2,1)} %bitcast.109, bf16[2,384,1024]{2,1,0:T(8,128)(2,1)} %bitcast.111, bf16[384,2048]{1,0:T(8,128)(2,1)} %get-tuple-element.88.flat_ref), custom_call_target="tpu_custom_call" | custom-call | flops 3221225472 | bytes 8388608 | tf_op jit(solution)/shard_map/pallas_call | solution.py:189
  317.7 3.5 collective-permute-start.27
  321.2 2.3 collective-permute-start.26
  323.5 2.9 collective-permute-start.25
  326.4 3.0 collective-permute-start.24
  329.4 12.2 %shard_map.102 = (bf16[2,1024,4,512]{3,2,1,0:T(4,128)(2,1)}, bf16[2,1024,4,512]{3,2,1,0:T(4,128)(2,1)}) custom-call(f32[1,1]{1,0:T(1,128)} %bitcast.16.scale_ref, bf16[2,384,1024]{2,1,0:T(8,128)(2,1)} %bitcast.110, bf16[2,384,1024]{2,1,0:T(8,128)(2,1)} %bitcast.112, ...), custom_call_target="tpu_custom_call", output_to_operand_aliasing={{0}: (4, {}), {1}: (5, {})} | custom-call | flops 3221225472 | bytes 8388608 | tf_op jit(solution)/shard_map/pallas_call | solution.py:189
  341.6 12.1 %collective-permute-done.25 = f32[96,512]{1,0:T(8,128)S(1)} collective-permute-done((f32[96,512]{1,0:T(8,128)S(1)}, f32[96,512]{1,0:T(8,128)S(1)}, u32[]{:S(2)}, u32[]{:S(2)}) %collective-permute-start.25) | collective-permute-done | bytes 196640 | tf_op jit(solution)/shard_map/ppermute | solution.py:252
  353.7 3.4 collective-permute-done.24
  (127 shorter events, 31.2 us)
Async XLA Ops:
  0.6 2.2 slice-start
  6.2 2.2 slice-start.2
  18.7 19.5 %all-to-all-start = ((f32[8,32,512]{2,1,0:T(8,128)}), f32[8,32,512]{2,1,0:T(8,128)S(1)}, u32[]{:S(2)}, u32[]{:S(2)}) async-start(f32[8,32,512]{2,1,0:T(8,128)} %bitcast.121), calls=%async_computation | async-start | bytes 1048576 | tf_op jit(solution)/shard_map/all_to_all | solution.py:216
  24.4 2.2 slice-start.1
  38.2 6.6 %collective-permute-start = (f32[32,512]{1,0:T(8,128)S(1)}, f32[32,512]{1,0:T(8,128)S(1)}, u32[]{:S(2)}, u32[]{:S(2)}) collective-permute-start(f32[32,512]{1,0:T(8,128)S(1)} %reduce_sum.99), channel_id=1, source_target_pairs={{0,0},{1,8},{2,16},{3,24},{4,1},{5,9},{6,17},{7,25},{8,2},{9,10},{... | collective-permute-start | bytes 196616 | tf_op jit(solution)/shard_map/ppermute | solution.py:228
  44.9 8.4 %copy-start.7 = (f32[32,512]{1,0:T(8,128)}, f32[32,512]{1,0:T(8,128)S(1)}, u32[]{:S(2)}) copy-start(f32[32,512]{1,0:T(8,128)S(1)} %collective-permute-done.refs_8_) | copy-start | bytes 196612
  44.9 8.2 %collective-permute-start.3 = (f32[32,512]{1,0:T(8,128)S(1)}, f32[32,512]{1,0:T(8,128)S(1)}, u32[]{:S(2)}, u32[]{:S(2)}) collective-permute-start(f32[32,512]{1,0:T(8,128)S(1)} %collective-permute-done.refs_8_), channel_id=1, source_target_pairs={{0,24},{8,0},{16,8},{24,16},{1,25},{9,1},{17,9},{25,17},{2,26},{10... | collective-permute-start | bytes 196616 | tf_op jit(solution)/shard_map/ppermute | solution.py:235
  47.6 5.4 %collective-permute-start.2 = (f32[32,512]{1,0:T(8,128)S(1)}, f32[32,512]{1,0:T(8,128)S(1)}, u32[]{:S(2)}, u32[]{:S(2)}) collective-permute-start(f32[32,512]{1,0:T(8,128)S(1)} %collective-permute-done.refs_8_), channel_id=1, source_target_pairs={{0,16},{8,24},{16,0},{24,8},{1,17},{9,25},{17,1},{25,9},{2,18},{10... | collective-permute-start | bytes 196616 | tf_op jit(solution)/shard_map/ppermute | solution.py:235
  50.7 2.6 collective-permute-start.1
  53.0 0.6 copy-start.13
  63.8 15.5 %all-to-all-start.1 = ((f32[8,32,512]{2,1,0:T(8,128)}), f32[8,32,512]{2,1,0:T(8,128)S(1)}, u32[]{:S(2)}, u32[]{:S(2)}) async-start(f32[8,32,512]{2,1,0:T(8,128)} %bitcast.118), calls=%async_computation.1 | async-start | bytes 1048576 | tf_op jit(solution)/shard_map/all_to_all | solution.py:216
  67.3 2.2 slice-start.3
  79.4 6.8 %collective-permute-start.4 = (f32[32,512]{1,0:T(8,128)S(1)}, f32[32,512]{1,0:T(8,128)S(1)}, u32[]{:S(2)}, u32[]{:S(2)}) collective-permute-start(f32[32,512]{1,0:T(8,128)S(1)} %reduce_sum.100), channel_id=1, source_target_pairs={{0,0},{1,8},{2,16},{3,24},{4,1},{5,9},{6,17},{7,25},{8,2},{9,10},{... | collective-permute-start | bytes 196616 | tf_op jit(solution)/shard_map/ppermute | solution.py:228
  86.2 9.0 %copy-start.10 = (f32[32,512]{1,0:T(8,128)}, f32[32,512]{1,0:T(8,128)S(1)}, u32[]{:S(2)}) copy-start(f32[32,512]{1,0:T(8,128)S(1)} %collective-permute-done.4.refs_9_) | copy-start | bytes 196612
  86.2 8.8 %collective-permute-start.7 = (f32[32,512]{1,0:T(8,128)S(1)}, f32[32,512]{1,0:T(8,128)S(1)}, u32[]{:S(2)}, u32[]{:S(2)}) collective-permute-start(f32[32,512]{1,0:T(8,128)S(1)} %collective-permute-done.4.refs_9_), channel_id=1, source_target_pairs={{0,24},{8,0},{16,8},{24,16},{1,25},{9,1},{17,9},{25,17},{2,26},{10... | collective-permute-start | bytes 196616 | tf_op jit(solution)/shard_map/ppermute | solution.py:235
  89.7 5.2 %collective-permute-start.6 = (f32[32,512]{1,0:T(8,128)S(1)}, f32[32,512]{1,0:T(8,128)S(1)}, u32[]{:S(2)}, u32[]{:S(2)}) collective-permute-start(f32[32,512]{1,0:T(8,128)S(1)} %collective-permute-done.4.refs_9_), channel_id=1, source_target_pairs={{0,16},{8,24},{16,0},{24,8},{1,17},{9,25},{17,1},{25,9},{2,18},{10... | collective-permute-start | bytes 196616 | tf_op jit(solution)/shard_map/ppermute | solution.py:235
  92.6 2.6 collective-permute-start.5
  94.9 0.6 copy-start.17
  94.9 0.6 copy-start.21
  95.2 0.6 copy-start.25
  121.7 6.6 %collective-permute-start.8 = (f32[32,512]{1,0:T(8,128)S(1)}, f32[32,512]{1,0:T(8,128)S(1)}, u32[]{:S(2)}, u32[]{:S(2)}) collective-permute-start(f32[32,512]{1,0:T(8,128)S(1)} %reduce_sum.101), channel_id=1, source_target_pairs={{0,0},{1,8},{2,16},{3,24},{4,1},{5,9},{6,17},{7,25},{8,2},{9,10},{... | collective-permute-start | bytes 196616 | tf_op jit(solution)/shard_map/ppermute | solution.py:228
  128.3 8.9 %copy-start.11 = (f32[32,512]{1,0:T(8,128)}, f32[32,512]{1,0:T(8,128)S(1)}, u32[]{:S(2)}) copy-start(f32[32,512]{1,0:T(8,128)S(1)} %collective-permute-done.8.refs_9_) | copy-start | bytes 196612
  128.3 8.6 %collective-permute-start.11 = (f32[32,512]{1,0:T(8,128)S(1)}, f32[32,512]{1,0:T(8,128)S(1)}, u32[]{:S(2)}, u32[]{:S(2)}) collective-permute-start(f32[32,512]{1,0:T(8,128)S(1)} %collective-permute-done.8.refs_9_), channel_id=1, source_target_pairs={{0,24},{8,0},{16,8},{24,16},{1,25},{9,1},{17,9},{25,17},{2,26},{10... | collective-permute-start | bytes 196616 | tf_op jit(solution)/shard_map/ppermute | solution.py:235
  132.0 5.0 %collective-permute-start.10 = (f32[32,512]{1,0:T(8,128)S(1)}, f32[32,512]{1,0:T(8,128)S(1)}, u32[]{:S(2)}, u32[]{:S(2)}) collective-permute-start(f32[32,512]{1,0:T(8,128)S(1)} %collective-permute-done.8.refs_9_), channel_id=1, source_target_pairs={{0,16},{8,24},{16,0},{24,8},{1,17},{9,25},{17,1},{25,9},{2,18},{10... | collective-permute-start | bytes 196616 | tf_op jit(solution)/shard_map/ppermute | solution.py:235
  134.6 2.6 collective-permute-start.9
  137.0 0.6 copy-start.18
  137.0 0.6 copy-start.22
  137.2 0.6 copy-start.26
  163.8 6.6 %collective-permute-start.12 = (f32[32,512]{1,0:T(8,128)S(1)}, f32[32,512]{1,0:T(8,128)S(1)}, u32[]{:S(2)}, u32[]{:S(2)}) collective-permute-start(f32[32,512]{1,0:T(8,128)S(1)} %reduce_sum.102), channel_id=1, source_target_pairs={{0,0},{1,8},{2,16},{3,24},{4,1},{5,9},{6,17},{7,25},{8,2},{9,10},{... | collective-permute-start | bytes 196616 | tf_op jit(solution)/shard_map/ppermute | solution.py:228
  170.3 8.9 %copy-start.9 = (f32[32,512]{1,0:T(8,128)}, f32[32,512]{1,0:T(8,128)S(1)}, u32[]{:S(2)}) copy-start(f32[32,512]{1,0:T(8,128)S(1)} %collective-permute-done.12.refs_9_) | copy-start | bytes 196612
  170.3 8.6 %collective-permute-start.15 = (f32[32,512]{1,0:T(8,128)S(1)}, f32[32,512]{1,0:T(8,128)S(1)}, u32[]{:S(2)}, u32[]{:S(2)}) collective-permute-start(f32[32,512]{1,0:T(8,128)S(1)} %collective-permute-done.12.refs_9_), channel_id=1, source_target_pairs={{0,24},{8,0},{16,8},{24,16},{1,25},{9,1},{17,9},{25,17},{2,26},{10... | collective-permute-start | bytes 196616 | tf_op jit(solution)/shard_map/ppermute | solution.py:235
  174.0 5.0 %collective-permute-start.14 = (f32[32,512]{1,0:T(8,128)S(1)}, f32[32,512]{1,0:T(8,128)S(1)}, u32[]{:S(2)}, u32[]{:S(2)}) collective-permute-start(f32[32,512]{1,0:T(8,128)S(1)} %collective-permute-done.12.refs_9_), channel_id=1, source_target_pairs={{0,16},{8,24},{16,0},{24,8},{1,17},{9,25},{17,1},{25,9},{2,18},{10... | collective-permute-start | bytes 196616 | tf_op jit(solution)/shard_map/ppermute | solution.py:235
  176.6 2.6 collective-permute-start.13
  179.0 0.6 copy-start.20
  189.8 15.6 %all-to-all-start.4 = ((f32[8,32,512]{2,1,0:T(8,128)}), f32[8,32,512]{2,1,0:T(8,128)}, u32[]{:S(2)}, u32[]{:S(2)}) async-start(f32[8,32,512]{2,1,0:T(8,128)} %bitcast.117), calls=%async_computation.4 | async-start | bytes 1048576 | tf_op jit(solution)/shard_map/all_to_all | solution.py:216
  193.9 2.8 copy-start
  200.1 10.6 %copy-start.4 = (bf16[2,6,64,1024]{3,2,1,0:T(8,128)(2,1)S(1)}, bf16[2,6,64,1024]{3,2,1,0:T(8,128)(2,1)}, u32[]{:S(2)}) copy-start(bf16[2,6,64,1024]{3,2,1,0:T(8,128)(2,1)} %param.11) | copy-start | bytes 4718596
  206.5 45.5 %all-to-all-start.5 = ((f32[8,64,512]{2,1,0:T(8,128)}), f32[8,64,512]{2,1,0:T(8,128)}, u32[]{:S(2)}, u32[]{:S(2)}) async-start(f32[8,64,512]{2,1,0:T(8,128)} %bitcast.8), calls=%async_computation.5 | async-start | bytes 2097152 | tf_op jit(solution)/shard_map/all_to_all | solution.py:216
  210.8 2.4 copy-start.3
  210.9 27.7 %collective-permute-start.16 = (f32[32,512]{1,0:T(8,128)S(1)}, f32[32,512]{1,0:T(8,128)S(1)}, u32[]{:S(2)}, u32[]{:S(2)}) collective-permute-start(f32[32,512]{1,0:T(8,128)S(1)} %reduce_sum.103), channel_id=1, source_target_pairs={{0,0},{1,8},{2,16},{3,24},{4,1},{5,9},{6,17},{7,25},{8,2},{9,10},{... | collective-permute-start | bytes 196616 | tf_op jit(solution)/shard_map/ppermute | solution.py:228
  238.6 4.8 %copy-start.8 = (f32[32,512]{1,0:T(8,128)}, f32[32,512]{1,0:T(8,128)S(1)}, u32[]{:S(2)}) copy-start(f32[32,512]{1,0:T(8,128)S(1)} %collective-permute-done.16.refs_9_) | copy-start | bytes 196612
  238.6 4.3 %collective-permute-start.19 = (f32[32,512]{1,0:T(8,128)S(1)}, f32[32,512]{1,0:T(8,128)S(1)}, u32[]{:S(2)}, u32[]{:S(2)}) collective-permute-start(f32[32,512]{1,0:T(8,128)S(1)} %collective-permute-done.16.refs_9_), channel_id=1, source_target_pairs={{0,24},{8,0},{16,8},{24,16},{1,25},{9,1},{17,9},{25,17},{2,26},{10... | collective-permute-start | bytes 196616 | tf_op jit(solution)/shard_map/ppermute | solution.py:235
  239.3 4.1 %collective-permute-start.18 = (f32[32,512]{1,0:T(8,128)S(1)}, f32[32,512]{1,0:T(8,128)S(1)}, u32[]{:S(2)}, u32[]{:S(2)}) collective-permute-start(f32[32,512]{1,0:T(8,128)S(1)} %collective-permute-done.16.refs_9_), channel_id=1, source_target_pairs={{0,16},{8,24},{16,0},{24,8},{1,17},{9,25},{17,1},{25,9},{2,18},{10... | collective-permute-start | bytes 196616 | tf_op jit(solution)/shard_map/ppermute | solution.py:235
  239.3 4.1 %collective-permute-start.17 = (f32[32,512]{1,0:T(8,128)S(1)}, f32[32,512]{1,0:T(8,128)S(1)}, u32[]{:S(2)}, u32[]{:S(2)}) collective-permute-start(f32[32,512]{1,0:T(8,128)S(1)} %collective-permute-done.16.refs_9_), channel_id=1, source_target_pairs={{0,8},{8,16},{16,24},{24,0},{1,9},{9,17},{17,25},{25,1},{2,10},{10... | collective-permute-start | bytes 196616 | tf_op jit(solution)/shard_map/ppermute | solution.py:235
  242.9 0.6 copy-start.14
  243.4 0.6 copy-start.23
  252.0 10.0 %all-to-all-start.6 = ((f32[8,16,512]{2,1,0:T(8,128)}), f32[8,16,512]{2,1,0:T(8,128)S(1)}, u32[]{:S(2)}, u32[]{:S(2)}) async-start(f32[8,16,512]{2,1,0:T(8,128)} %bitcast.122), calls=%async_computation.6 | async-start | bytes 524288 | tf_op jit(solution)/shard_map/all_to_all | solution.py:216
  259.2 17.0 %copy-start.2 = (bf16[384,2048]{1,0:T(8,128)(2,1)S(1)}, bf16[384,2048]{1,0:T(8,128)(2,1)}, u32[]{:S(2)}) copy-start(bf16[384,2048]{1,0:T(8,128)(2,1)} %get-tuple-element.88.flat_ref) | copy-start | bytes 4718596
  259.2 17.0 %copy-start.6 = (f32[384,384]{1,0:T(8,128)S(1)}, f32[384,384]{1,0:T(8,128)}, u32[]{:S(2)}) copy-start(f32[384,384]{1,0:T(8,128)} %convolution_add_fusion) | copy-start | bytes 1769476
  262.1 7.2 %collective-permute-start.20 = (f32[16,512]{1,0:T(8,128)S(1)}, f32[16,512]{1,0:T(8,128)S(1)}, u32[]{:S(2)}, u32[]{:S(2)}) collective-permute-start(f32[16,512]{1,0:T(8,128)S(1)} %reduce_sum.104), channel_id=1, source_target_pairs={{0,0},{1,8},{2,16},{3,24},{4,1},{5,9},{6,17},{7,25},{8,2},{9,10},{... | collective-permute-start | bytes 98312 | tf_op jit(solution)/shard_map/ppermute | solution.py:228
  269.3 8.6 %copy-start.27 = (f32[16,512]{1,0:T(8,128)}, f32[16,512]{1,0:T(8,128)S(1)}, u32[]{:S(2)}) copy-start(f32[16,512]{1,0:T(8,128)S(1)} %collective-permute-done.20.refs_4_) | copy-start | bytes 98308
  269.3 8.7 %collective-permute-start.23 = (f32[16,512]{1,0:T(8,128)S(1)}, f32[16,512]{1,0:T(8,128)S(1)}, u32[]{:S(2)}, u32[]{:S(2)}) collective-permute-start(f32[16,512]{1,0:T(8,128)S(1)} %collective-permute-done.20.refs_4_), channel_id=1, source_target_pairs={{0,24},{8,0},{16,8},{24,16},{1,25},{9,1},{17,9},{25,17},{2,26},{10... | collective-permute-start | bytes 98312 | tf_op jit(solution)/shard_map/ppermute | solution.py:235
  273.8 4.2 %collective-permute-start.22 = (f32[16,512]{1,0:T(8,128)S(1)}, f32[16,512]{1,0:T(8,128)S(1)}, u32[]{:S(2)}, u32[]{:S(2)}) collective-permute-start(f32[16,512]{1,0:T(8,128)S(1)} %collective-permute-done.20.refs_4_), channel_id=1, source_target_pairs={{0,16},{8,24},{16,0},{24,8},{1,17},{9,25},{17,1},{25,9},{2,18},{10... | collective-permute-start | bytes 98312 | tf_op jit(solution)/shard_map/ppermute | solution.py:235
  276.1 1.9 collective-permute-start.21
  277.9 0.6 copy-start.29
  281.0 2.7 copy-start.1
  281.0 2.8 copy-start.5
  287.4 10.9 %all-to-all-start.7 = ((f32[32,8,128]{2,1,0:T(8,128)}), f32[32,8,128]{2,1,0:T(8,128)S(1)}, u32[]{:S(2)}, u32[]{:S(2)}) async-start(f32[32,8,128]{2,1,0:T(8,128)} %broadcast_in_dim.3), calls=%async_computation.7 | async-start | bytes 262144 | tf_op jit(solution)/shard_map/all_to_all | solution.py:340
  299.7 17.9 %all-to-all-start.8 = ((f32[8,32,512]{2,1,0:T(8,128)}), f32[8,32,512]{2,1,0:T(8,128)S(1)}, u32[]{:S(2)}, u32[]{:S(2)}) async-start(f32[8,32,512]{2,1,0:T(8,128)} %bitcast.19), calls=%async_computation.8 | async-start | bytes 1048576 | tf_op jit(solution)/shard_map/all_to_all | solution.py:216
  317.7 23.9 %collective-permute-start.27 = (f32[96,512]{1,0:T(8,128)S(1)}, f32[96,512]{1,0:T(8,128)S(1)}, u32[]{:S(2)}, u32[]{:S(2)}) collective-permute-start(f32[96,512]{1,0:T(8,128)S(1)} %pad_maximum_fusion.3), channel_id=1, source_target_pairs={{0,24},{1,0},{2,8},{3,16},{4,25},{5,1},{6,9},{7,17},{8,26},{9,2},{... | collective-permute-start | bytes 589832 | tf_op jit(solution)/shard_map/ppermute | solution.py:252
  321.2 20.4 %collective-permute-start.26 = (f32[96,512]{1,0:T(8,128)S(1)}, f32[96,512]{1,0:T(8,128)S(1)}, u32[]{:S(2)}, u32[]{:S(2)}) collective-permute-start(f32[96,512]{1,0:T(8,128)S(1)} %pad_maximum_fusion.3), channel_id=1, source_target_pairs={{0,16},{1,24},{2,0},{3,8},{4,17},{5,25},{6,1},{7,9},{8,18},{9,26},... | collective-permute-start | bytes 589832 | tf_op jit(solution)/shard_map/ppermute | solution.py:252
  323.5 30.2 %collective-permute-start.25 = (f32[96,512]{1,0:T(8,128)S(1)}, f32[96,512]{1,0:T(8,128)S(1)}, u32[]{:S(2)}, u32[]{:S(2)}) collective-permute-start(f32[96,512]{1,0:T(8,128)S(1)} %pad_maximum_fusion.3), channel_id=1, source_target_pairs={{0,8},{1,16},{2,24},{3,0},{4,9},{5,17},{6,25},{7,1},{8,10},{9,18},... | collective-permute-start | bytes 589832 | tf_op jit(solution)/shard_map/ppermute | solution.py:252
  326.4 30.7 %collective-permute-start.24 = (f32[96,512]{1,0:T(8,128)S(1)}, f32[96,512]{1,0:T(8,128)S(1)}, u32[]{:S(2)}, u32[]{:S(2)}) collective-permute-start(f32[96,512]{1,0:T(8,128)S(1)} %pad_maximum_fusion.3), channel_id=1, source_target_pairs={{0,0},{1,8},{2,16},{3,24},{4,1},{5,9},{6,17},{7,25},{8,2},{9,10},{... | collective-permute-start | bytes 589832 | tf_op jit(solution)/shard_map/ppermute | solution.py:252
  357.4 0.9 copy-start.31
  (7 other events, 4.3 us)

commit v2 on v1

--- a/solution.py
+++ b/solution.py
@@ -237,20 +237,10 @@
     ]
 
 
-def gather_direct(mine):
+def gather_ordered(mine):
     rows = lax.axis_size("row")
-    cols = lax.axis_size("col")
-    ratio = cols // rows
     here = lax.axis_index("row")
-    parts = []
-    for s in range(rows):
-        moves = [
-            (r * cols + k, (k + s) % rows * cols + ratio * r + k // rows)
-            for r in range(rows)
-            for k in range(cols)
-        ]
-        parts.append(lax.ppermute(mine, ("row", "col"), moves))
-    parts = jnp.stack(parts)
+    parts = jnp.stack(gather(mine))
     return [
         lax.dynamic_index_in_dim(parts, (here - i) % rows, 0, keepdims=False) for i in range(rows)
     ]
@@ -350,7 +340,7 @@
         if l == layers - 1:
             rest, *out = lax.optimization_barrier((rest, *out))
             mine = jnp.concatenate([jnp.sum(bulk, axis=0), jnp.sum(rest, axis=0)])
-            parts = gather_direct(mine)
+            parts = gather_ordered(mine)
     rows = lax.axis_size("row")
     count = (steps - CUT) * batch // rows
     input_grad = jnp.concatenate([p[count:] for p in parts] + [p[:count] for p in parts])

time: 360 us -> 350 us (0.972)
  starting transfers between devices: 88.1 us -> 82.8 us
  waiting for transfers between devices: 101 us -> 96.3 us
    ppermute x4 -> x0, waiting for transfers between devices: 15.6 us -> none  [gather_direct(): parts.append(lax.ppermute(mine, ('row', 'col'), moves))]
    ppermute x4 -> x0, starting transfers between devices: 11.7 us -> none  [gather_direct(): parts.append(lax.ppermute(mine, ('row', 'col'), moves))]
    ppermute x6 -> x7, waiting for transfers between devices: 46.1 us -> 56.8 us  [place(): return lax.ppermute(mine, ('row', 'col'), moves)]
    ppermute x18 -> x21, starting transfers between devices: 34 us -> 37.7 us  [gather(): lax.ppermute(mine, 'row', [(i, (i + s) % rows) for i in range(rows)])]
    ppermute x6 -> x7, starting transfers between devices: 12.7 us -> 15.5 us  [place(): return lax.ppermute(mine, ('row', 'col'), moves)]
    ppermute x18 -> x21, waiting for transfers between devices: 12.3 us -> 12.3 us  [gather(): lax.ppermute(mine, 'row', [(i, (i + s) % rows) for i in range(rows)])]
  transfers between devices with their start and end apart: 35 -> 35, of which waited for: 24 -> 23; matrix products, arithmetic and copies ran while one was open for 7% -> 7% of each run, Pallas kernels for 9% -> 9%
where the time goes in v2:
time: 350 us; the launch traced here: 348 us
  waiting for transfers between devices  96.3 us (28%)
  starting transfers between devices  82.8 us (24%)
  Pallas kernels  81.5 us (23%)
  blocking collectives  31.8 us (9%)
  local copies, waits for them, and re-layouts  27.9 us (8%)
  matrix products  19.5 us (6%)
  other arithmetic  5.17 us (1%)
    pallas_call x7, Pallas kernels, run_step(): pl.pallas_call(functools.partial(step_kernel, plan, [[which for which, _...  57.2 us
    ppermute x7, waiting for transfers between devices, place(): return lax.ppermute(mine, ('row', 'col'), moves)  56.8 us
    ppermute x21, starting transfers between devices, gather(): lax.ppermute(mine, 'row', [(i, (i + s) % rows) for i in range(rows)])  37.7 us
    all_to_all x2, blocking collectives, swap(): return lax.all_to_all(pieces, 'col', 0, 0, tiled=True)  31.8 us
    all_to_all x6, starting transfers between devices, swap(): return lax.all_to_all(pieces, 'col', 0, 0, tiled=True)  25.9 us
    pallas_call x2, Pallas kernels, layer_grads(): pl.pallas_call(grads_kernel_keep if before else grads_kernel, grid=(rows...  24.3 us
    all_to_all x6, waiting for transfers between devices, swap(): return lax.all_to_all(pieces, 'col', 0, 0, tiled=True)  23.3 us
    unnamed x75, local copies, waits for them, and re-layouts  18.2 us
  transfers between devices with their start and end apart: 35, of which 23 were waited for; matrix products, arithmetic and copies ran while one was open for 7% of the time, Pallas kernels for 9%

profile of v2, /device:TPU:5, one launch (start us, length us, event | category | flops | bytes accessed | tf_op | source)
XLA Modules:
  0.0 348.1 jit_solution(6904357249089319020)
XLA Ops:
  0.6 2.2 slice-done
  2.8 3.4 copy.24
  6.2 2.2 slice-done.2
  8.4 3.4 copy.25
  11.8 6.9 %shard_map.94 = (bf16[384,2048]{1,0:T(8,128)(2,1)}, f32[64,512]{1,0:T(8,128)}, f32[2,128,512]{2,1,0:T(8,128)}) custom-call(f32[2,6,64,4,512]{4,3,2,1,0:T(4,128)} %refs_0_.13, f32[2,7,64,512]{3,2,1,0:T(8,128)} %refs_2_.13, f32[2,7,64,512]{3,2,1,0:T(8,128)} %refs_2_.13, f32[6,64,512]{2,1,0:T(8,128)} %refs_4_.9, bf16[1024,2048]{1,0:T(8,128)(2,1)} %bitcast.96, ...), custom_call_target="tpu_custom_call" | custom-call | flops 536871936 | bytes 9388608 | tf_op jit(solution)/shard_map/pallas_call | solution.py:137
  18.7 5.8 %all-to-all-start = ((f32[8,32,512]{2,1,0:T(8,128)}), f32[8,32,512]{2,1,0:T(8,128)S(1)}, u32[]{:S(2)}, u32[]{:S(2)}) async-start(f32[8,32,512]{2,1,0:T(8,128)} %bitcast.121), calls=%async_computation | async-start | bytes 1048576 | tf_op jit(solution)/shard_map/all_to_all | solution.py:216
  24.4 2.2 slice-done.1
  26.6 3.4 copy.26
  30.0 8.2 %all-to-all-done = f32[8,32,512]{2,1,0:T(8,128)S(1)} async-done(((f32[8,32,512]{2,1,0:T(8,128)}), f32[8,32,512]{2,1,0:T(8,128)S(1)}, u32[]{:S(2)}, u32[]{:S(2)}) %all-to-all-start) | async-done | bytes 524320 | tf_op jit(solution)/shard_map/all_to_all | solution.py:216
  38.2 1.9 collective-permute-start
  40.2 4.7 %collective-permute-done.refs_8_ = f32[32,512]{1,0:T(8,128)S(1)} collective-permute-done((f32[32,512]{1,0:T(8,128)S(1)}, f32[32,512]{1,0:T(8,128)S(1)}, u32[]{:S(2)}, u32[]{:S(2)}) %collective-permute-start) | collective-permute-done | bytes 65568 | tf_op jit(solution)/shard_map/ppermute | solution.py:228
  44.9 2.7 collective-permute-start.3
  47.6 3.1 collective-permute-start.2
  50.7 2.4 collective-permute-done.3.refs_11_
  53.9 9.9 %shard_map.95 = (bf16[384,2048]{1,0:T(8,128)(2,1)}, f32[64,512]{1,0:T(8,128)}, bf16[384,2048]{1,0:T(8,128)(2,1)}, f32[64,512]{1,0:T(8,128)}, f32[2,128,512]{2,1,0:T(8,128)}) custom-call(f32[2,6,64,4,512]{4,3,2,1,0:T(4,128)} %refs_0_.13, f32[2,7,64,512]{3,2,1,0:T(8,128)} %refs_2_.13, f32[2,7,64,512]{3,2,1,0:T(8,128)} %refs_2_.13, ...), custom_call_target="tpu_custom_call", output_to_operand_aliasing={{0}: (16, {})} | custom-call | flops 805307392 | bytes 13582912 | tf_op jit(solution)/shard_map/pallas_call | solution.py:137
  63.8 3.5 all-to-all-start.1
  67.3 2.2 slice-done.3
  69.5 3.3 copy.27
  72.8 6.5 %all-to-all-done.1 = f32[8,32,512]{2,1,0:T(8,128)S(1)} async-done(((f32[8,32,512]{2,1,0:T(8,128)}), f32[8,32,512]{2,1,0:T(8,128)S(1)}, u32[]{:S(2)}, u32[]{:S(2)}) %all-to-all-start.1) | async-done | bytes 524320 | tf_op jit(solution)/shard_map/all_to_all | solution.py:216
  79.4 1.9 collective-permute-start.4
  81.3 4.9 %collective-permute-done.4.refs_9_ = f32[32,512]{1,0:T(8,128)S(1)} collective-permute-done((f32[32,512]{1,0:T(8,128)S(1)}, f32[32,512]{1,0:T(8,128)S(1)}, u32[]{:S(2)}, u32[]{:S(2)}) %collective-permute-start.4) | collective-permute-done | bytes 65568 | tf_op jit(solution)/shard_map/ppermute | solution.py:228
  86.2 3.5 %collective-permute-start.7 = (f32[32,512]{1,0:T(8,128)S(1)}, f32[32,512]{1,0:T(8,128)S(1)}, u32[]{:S(2)}, u32[]{:S(2)}) collective-permute-start(f32[32,512]{1,0:T(8,128)S(1)} %collective-permute-done.4.refs_9_), channel_id=1, source_target_pairs={{0,24},{8,0},{16,8},{24,16},{1,25},{9,1},{17,9},{25,17},{2,26},{10... | collective-permute-start | bytes 196616 | tf_op jit(solution)/shard_map/ppermute | solution.py:235
  89.7 2.9 collective-permute-start.6
  92.6 2.4 collective-permute-done.7.refs_12_
  95.8 10.0 %shard_map.96 = (bf16[384,2048]{1,0:T(8,128)(2,1)}, f32[64,512]{1,0:T(8,128)}, bf16[384,2048]{1,0:T(8,128)(2,1)}, f32[64,512]{1,0:T(8,128)}, f32[2,128,512]{2,1,0:T(8,128)}) custom-call(f32[2,6,64,4,512]{4,3,2,1,0:T(4,128)} %refs_0_.13, f32[2,7,64,512]{3,2,1,0:T(8,128)} %refs_2_.13, ...), custom_call_target="tpu_custom_call", output_to_operand_aliasing={{0}: (17, {}), {2}: (18, {})} | custom-call | flops 805307392 | bytes 13582912 | tf_op jit(solution)/shard_map/pallas_call | solution.py:137
  105.8 15.9 %all_to_all.45 = f32[8,32,512]{2,1,0:T(8,128)S(1)} all-to-all(f32[8,32,512]{2,1,0:T(8,128)} %bitcast.119), channel_id=1, replica_groups=mesh['row'=4,'col'=8] {'col'}, dimensions={0} | all-to-all | bytes 1048576 | tf_op jit(solution)/shard_map/all_to_all | solution.py:216
  121.7 1.9 collective-permute-start.8
  123.7 4.7 %collective-permute-done.8.refs_9_ = f32[32,512]{1,0:T(8,128)S(1)} collective-permute-done((f32[32,512]{1,0:T(8,128)S(1)}, f32[32,512]{1,0:T(8,128)S(1)}, u32[]{:S(2)}, u32[]{:S(2)}) %collective-permute-start.8) | collective-permute-done | bytes 65568 | tf_op jit(solution)/shard_map/ppermute | solution.py:228
  128.3 3.6 %collective-permute-start.11 = (f32[32,512]{1,0:T(8,128)S(1)}, f32[32,512]{1,0:T(8,128)S(1)}, u32[]{:S(2)}, u32[]{:S(2)}) collective-permute-start(f32[32,512]{1,0:T(8,128)S(1)} %collective-permute-done.8.refs_9_), channel_id=1, source_target_pairs={{0,24},{8,0},{16,8},{24,16},{1,25},{9,1},{17,9},{25,17},{2,26},{10... | collective-permute-start | bytes 196616 | tf_op jit(solution)/shard_map/ppermute | solution.py:235
  132.0 2.7 collective-permute-start.10
  134.6 2.4 collective-permute-done.11.refs_12_
  137.8 10.0 %shard_map.97 = (bf16[384,2048]{1,0:T(8,128)(2,1)}, f32[64,512]{1,0:T(8,128)}, bf16[384,2048]{1,0:T(8,128)(2,1)}, f32[64,512]{1,0:T(8,128)}, f32[2,128,512]{2,1,0:T(8,128)}) custom-call(f32[2,6,64,4,512]{4,3,2,1,0:T(4,128)} %refs_0_.13, f32[2,7,64,512]{3,2,1,0:T(8,128)} %refs_2_.13, ...), custom_call_target="tpu_custom_call", output_to_operand_aliasing={{0}: (17, {}), {2}: (18, {})} | custom-call | flops 805307392 | bytes 13582912 | tf_op jit(solution)/shard_map/pallas_call | solution.py:137
  147.8 15.9 %all_to_all.46 = f32[8,32,512]{2,1,0:T(8,128)S(1)} all-to-all(f32[8,32,512]{2,1,0:T(8,128)} %bitcast.120), channel_id=1, replica_groups=mesh['row'=4,'col'=8] {'col'}, dimensions={0} | all-to-all | bytes 1048576 | tf_op jit(solution)/shard_map/all_to_all | solution.py:216
  165.7 4.7 %collective-permute-done.12.refs_9_ = f32[32,512]{1,0:T(8,128)S(1)} collective-permute-done((f32[32,512]{1,0:T(8,128)S(1)}, f32[32,512]{1,0:T(8,128)S(1)}, u32[]{:S(2)}, u32[]{:S(2)}) %collective-permute-start.12) | collective-permute-done | bytes 65568 | tf_op jit(solution)/shard_map/ppermute | solution.py:228
  170.3 3.6 %collective-permute-start.15 = (f32[32,512]{1,0:T(8,128)S(1)}, f32[32,512]{1,0:T(8,128)S(1)}, u32[]{:S(2)}, u32[]{:S(2)}) collective-permute-start(f32[32,512]{1,0:T(8,128)S(1)} %collective-permute-done.12.refs_9_), channel_id=1, source_target_pairs={{0,24},{8,0},{16,8},{24,16},{1,25},{9,1},{17,9},{25,17},{2,26},{10... | collective-permute-start | bytes 196616 | tf_op jit(solution)/shard_map/ppermute | solution.py:235
  174.0 2.7 collective-permute-start.14
  176.6 2.4 collective-permute-done.15.refs_12_
  179.9 10.0 %shard_map.98 = (bf16[384,2048]{1,0:T(8,128)(2,1)}, f32[64,512]{1,0:T(8,128)}, bf16[384,2048]{1,0:T(8,128)(2,1)}, f32[64,512]{1,0:T(8,128)}, f32[2,128,512]{2,1,0:T(8,128)}) custom-call(f32[2,6,64,4,512]{4,3,2,1,0:T(4,128)} %refs_0_.13, f32[2,7,64,512]{3,2,1,0:T(8,128)} %refs_2_.13, ...), custom_call_target="tpu_custom_call", output_to_operand_aliasing={{0}: (17, {}), {2}: (18, {})} | custom-call | flops 805307392 | bytes 13582912 | tf_op jit(solution)/shard_map/pallas_call | solution.py:137
  189.8 4.1 %all-to-all-start.4 = ((f32[8,32,512]{2,1,0:T(8,128)}), f32[8,32,512]{2,1,0:T(8,128)}, u32[]{:S(2)}, u32[]{:S(2)}) async-start(f32[8,32,512]{2,1,0:T(8,128)} %bitcast.117), calls=%async_computation.4 | async-start | bytes 1048576 | tf_op jit(solution)/shard_map/all_to_all | solution.py:216
  194.0 2.8 fusion.11
  196.7 2.3 fusion.8
  200.1 5.3 %all-to-all-done.4 = f32[8,32,512]{2,1,0:T(8,128)} async-done(((f32[8,32,512]{2,1,0:T(8,128)}), f32[8,32,512]{2,1,0:T(8,128)}, u32[]{:S(2)}, u32[]{:S(2)}) %all-to-all-start.4) | async-done | bytes 524320 | tf_op jit(solution)/shard_map/all_to_all | solution.py:216
  206.5 4.2 %all-to-all-start.5 = ((f32[8,64,512]{2,1,0:T(8,128)}), f32[8,64,512]{2,1,0:T(8,128)}, u32[]{:S(2)}, u32[]{:S(2)}) async-start(f32[8,64,512]{2,1,0:T(8,128)} %bitcast.8), calls=%async_computation.5 | async-start | bytes 2097152 | tf_op jit(solution)/shard_map/all_to_all | solution.py:216
  210.9 2.2 collective-permute-start.16
  213.3 25.3 %collective-permute-done.16.refs_9_ = f32[32,512]{1,0:T(8,128)S(1)} collective-permute-done((f32[32,512]{1,0:T(8,128)S(1)}, f32[32,512]{1,0:T(8,128)S(1)}, u32[]{:S(2)}, u32[]{:S(2)}) %collective-permute-start.16) | collective-permute-done | bytes 65568 | tf_op jit(solution)/shard_map/ppermute | solution.py:228
  244.0 8.0 %shard_map.99 = (bf16[384,2048]{1,0:T(8,128)(2,1)}, bf16[384,2048]{1,0:T(8,128)(2,1)}, f32[64,512]{1,0:T(8,128)}, f32[2,64,512]{2,1,0:T(8,128)}) custom-call(f32[2,6,64,4,512]{4,3,2,1,0:T(4,128)} %refs_0_.13, f32[2,7,64,512]{3,2,1,0:T(8,128)} %refs_2_.13, f32[2,7,64,512]{3,2,1,0:T(8,128)} %refs_2_.13, ...), custom_call_target="tpu_custom_call", output_to_operand_aliasing={{0}: (16, {}), {1}: (17, {})} | custom-call | flops 536871936 | bytes 9388608 | tf_op jit(solution)/shard_map/pallas_call | solution.py:137
  252.0 4.3 %all-to-all-start.6 = ((f32[8,16,512]{2,1,0:T(8,128)}), f32[8,16,512]{2,1,0:T(8,128)S(1)}, u32[]{:S(2)}, u32[]{:S(2)}) async-start(f32[8,16,512]{2,1,0:T(8,128)} %bitcast.122), calls=%async_computation.6 | async-start | bytes 524288 | tf_op jit(solution)/shard_map/all_to_all | solution.py:216
  259.2 2.8 all-to-all-done.6
  262.1 2.8 collective-permute-start.20
  264.9 2.5 convolution_add_fusion.1
  267.3 1.9 collective-permute-done.20.refs_4_
  269.3 4.5 %collective-permute-start.23 = (f32[16,512]{1,0:T(8,128)S(1)}, f32[16,512]{1,0:T(8,128)S(1)}, u32[]{:S(2)}, u32[]{:S(2)}) collective-permute-start(f32[16,512]{1,0:T(8,128)S(1)} %collective-permute-done.20.refs_4_), channel_id=1, source_target_pairs={{0,24},{8,0},{16,8},{24,16},{1,25},{9,1},{17,9},{25,17},{2,26},{10... | collective-permute-start | bytes 98312 | tf_op jit(solution)/shard_map/ppermute | solution.py:235
  273.8 2.3 collective-permute-start.22
  278.6 2.5 shard_map.100.flat_ref
  281.0 2.7 fusion.17
  287.4 3.7 %all-to-all-start.7 = ((f32[32,8,128]{2,1,0:T(8,128)}), f32[32,8,128]{2,1,0:T(8,128)S(1)}, u32[]{:S(2)}, u32[]{:S(2)}) async-start(f32[32,8,128]{2,1,0:T(8,128)} %broadcast_in_dim.3), calls=%async_computation.7 | async-start | bytes 262144 | tf_op jit(solution)/shard_map/all_to_all | solution.py:330
  291.1 2.4 fusion.14
  294.4 3.9 %all-to-all-done.7 = f32[32,8,128]{2,1,0:T(8,128)S(1)} async-done(((f32[32,8,128]{2,1,0:T(8,128)}), f32[32,8,128]{2,1,0:T(8,128)S(1)}, u32[]{:S(2)}, u32[]{:S(2)}) %all-to-all-start.7) | async-done | bytes 131104 | tf_op jit(solution)/shard_map/all_to_all | solution.py:330
  299.7 4.0 %all-to-all-start.8 = ((f32[8,32,512]{2,1,0:T(8,128)}), f32[8,32,512]{2,1,0:T(8,128)S(1)}, u32[]{:S(2)}, u32[]{:S(2)}) async-start(f32[8,32,512]{2,1,0:T(8,128)} %bitcast.19), calls=%async_computation.8 | async-start | bytes 1048576 | tf_op jit(solution)/shard_map/all_to_all | solution.py:216
  305.0 12.2 %shard_map.101 = (bf16[2,1024,4,512]{3,2,1,0:T(4,128)(2,1)}, bf16[2,1024,4,512]{3,2,1,0:T(4,128)(2,1)}) custom-call(f32[1,1]{1,0:T(1,128)} %bitcast.16.scale_ref, bf16[2,384,1024]{2,1,0:T(8,128)(2,1)} %bitcast.109, bf16[2,384,1024]{2,1,0:T(8,128)(2,1)} %bitcast.111, bf16[384,2048]{1,0:T(8,128)(2,1)} %get-tuple-element.88.flat_ref), custom_call_target="tpu_custom_call" | custom-call | flops 3221225472 | bytes 8388608 | tf_op jit(solution)/shard_map/pallas_call | solution.py:189
  317.7 2.8 collective-permute-start.24
  320.6 10.6 %collective-permute-done.24 = f32[96,512]{1,0:T(8,128)S(1)} collective-permute-done((f32[96,512]{1,0:T(8,128)S(1)}, f32[96,512]{1,0:T(8,128)S(1)}, u32[]{:S(2)}, u32[]{:S(2)}) %collective-permute-start.24) | collective-permute-done | bytes 196640 | tf_op jit(solution)/shard_map/ppermute | solution.py:228
  331.2 2.0 collective-permute-start.27
  334.8 12.2 %shard_map.102 = (bf16[2,1024,4,512]{3,2,1,0:T(4,128)(2,1)}, bf16[2,1024,4,512]{3,2,1,0:T(4,128)(2,1)}) custom-call(f32[1,1]{1,0:T(1,128)} %bitcast.16.scale_ref, bf16[2,384,1024]{2,1,0:T(8,128)(2,1)} %bitcast.110, bf16[2,384,1024]{2,1,0:T(8,128)(2,1)} %bitcast.112, ...), custom_call_target="tpu_custom_call", output_to_operand_aliasing={{0}: (4, {}), {1}: (5, {})} | custom-call | flops 3221225472 | bytes 8388608 | tf_op jit(solution)/shard_map/pallas_call | solution.py:189
  (127 shorter events, 27.0 us)
Async XLA Ops:
  0.6 2.2 slice-start
  6.2 2.2 slice-start.2
  18.7 19.5 %all-to-all-start = ((f32[8,32,512]{2,1,0:T(8,128)}), f32[8,32,512]{2,1,0:T(8,128)S(1)}, u32[]{:S(2)}, u32[]{:S(2)}) async-start(f32[8,32,512]{2,1,0:T(8,128)} %bitcast.121), calls=%async_computation | async-start | bytes 1048576 | tf_op jit(solution)/shard_map/all_to_all | solution.py:216
  24.4 2.2 slice-start.1
  38.2 6.6 %collective-permute-start = (f32[32,512]{1,0:T(8,128)S(1)}, f32[32,512]{1,0:T(8,128)S(1)}, u32[]{:S(2)}, u32[]{:S(2)}) collective-permute-start(f32[32,512]{1,0:T(8,128)S(1)} %reduce_sum.99), channel_id=1, source_target_pairs={{0,0},{1,8},{2,16},{3,24},{4,1},{5,9},{6,17},{7,25},{8,2},{9,10},{... | collective-permute-start | bytes 196616 | tf_op jit(solution)/shard_map/ppermute | solution.py:228
  44.9 8.4 %copy-start.7 = (f32[32,512]{1,0:T(8,128)}, f32[32,512]{1,0:T(8,128)S(1)}, u32[]{:S(2)}) copy-start(f32[32,512]{1,0:T(8,128)S(1)} %collective-permute-done.refs_8_) | copy-start | bytes 196612
  44.9 8.2 %collective-permute-start.3 = (f32[32,512]{1,0:T(8,128)S(1)}, f32[32,512]{1,0:T(8,128)S(1)}, u32[]{:S(2)}, u32[]{:S(2)}) collective-permute-start(f32[32,512]{1,0:T(8,128)S(1)} %collective-permute-done.refs_8_), channel_id=1, source_target_pairs={{0,24},{8,0},{16,8},{24,16},{1,25},{9,1},{17,9},{25,17},{2,26},{10... | collective-permute-start | bytes 196616 | tf_op jit(solution)/shard_map/ppermute | solution.py:235
  47.6 5.4 %collective-permute-start.2 = (f32[32,512]{1,0:T(8,128)S(1)}, f32[32,512]{1,0:T(8,128)S(1)}, u32[]{:S(2)}, u32[]{:S(2)}) collective-permute-start(f32[32,512]{1,0:T(8,128)S(1)} %collective-permute-done.refs_8_), channel_id=1, source_target_pairs={{0,16},{8,24},{16,0},{24,8},{1,17},{9,25},{17,1},{25,9},{2,18},{10... | collective-permute-start | bytes 196616 | tf_op jit(solution)/shard_map/ppermute | solution.py:235
  50.7 2.6 collective-permute-start.1
  53.0 0.6 copy-start.13
  63.8 15.5 %all-to-all-start.1 = ((f32[8,32,512]{2,1,0:T(8,128)}), f32[8,32,512]{2,1,0:T(8,128)S(1)}, u32[]{:S(2)}, u32[]{:S(2)}) async-start(f32[8,32,512]{2,1,0:T(8,128)} %bitcast.118), calls=%async_computation.1 | async-start | bytes 1048576 | tf_op jit(solution)/shard_map/all_to_all | solution.py:216
  67.3 2.2 slice-start.3
  79.4 6.8 %collective-permute-start.4 = (f32[32,512]{1,0:T(8,128)S(1)}, f32[32,512]{1,0:T(8,128)S(1)}, u32[]{:S(2)}, u32[]{:S(2)}) collective-permute-start(f32[32,512]{1,0:T(8,128)S(1)} %reduce_sum.100), channel_id=1, source_target_pairs={{0,0},{1,8},{2,16},{3,24},{4,1},{5,9},{6,17},{7,25},{8,2},{9,10},{... | collective-permute-start | bytes 196616 | tf_op jit(solution)/shard_map/ppermute | solution.py:228
  86.2 9.0 %copy-start.10 = (f32[32,512]{1,0:T(8,128)}, f32[32,512]{1,0:T(8,128)S(1)}, u32[]{:S(2)}) copy-start(f32[32,512]{1,0:T(8,128)S(1)} %collective-permute-done.4.refs_9_) | copy-start | bytes 196612
  86.2 8.8 %collective-permute-start.7 = (f32[32,512]{1,0:T(8,128)S(1)}, f32[32,512]{1,0:T(8,128)S(1)}, u32[]{:S(2)}, u32[]{:S(2)}) collective-permute-start(f32[32,512]{1,0:T(8,128)S(1)} %collective-permute-done.4.refs_9_), channel_id=1, source_target_pairs={{0,24},{8,0},{16,8},{24,16},{1,25},{9,1},{17,9},{25,17},{2,26},{10... | collective-permute-start | bytes 196616 | tf_op jit(solution)/shard_map/ppermute | solution.py:235
  89.7 5.2 %collective-permute-start.6 = (f32[32,512]{1,0:T(8,128)S(1)}, f32[32,512]{1,0:T(8,128)S(1)}, u32[]{:S(2)}, u32[]{:S(2)}) collective-permute-start(f32[32,512]{1,0:T(8,128)S(1)} %collective-permute-done.4.refs_9_), channel_id=1, source_target_pairs={{0,16},{8,24},{16,0},{24,8},{1,17},{9,25},{17,1},{25,9},{2,18},{10... | collective-permute-start | bytes 196616 | tf_op jit(solution)/shard_map/ppermute | solution.py:235
  92.6 2.6 collective-permute-start.5
  94.9 0.6 copy-start.17
  94.9 0.6 copy-start.21
  95.2 0.6 copy-start.25
  121.7 6.6 %collective-permute-start.8 = (f32[32,512]{1,0:T(8,128)S(1)}, f32[32,512]{1,0:T(8,128)S(1)}, u32[]{:S(2)}, u32[]{:S(2)}) collective-permute-start(f32[32,512]{1,0:T(8,128)S(1)} %reduce_sum.101), channel_id=1, source_target_pairs={{0,0},{1,8},{2,16},{3,24},{4,1},{5,9},{6,17},{7,25},{8,2},{9,10},{... | collective-permute-start | bytes 196616 | tf_op jit(solution)/shard_map/ppermute | solution.py:228
  128.3 8.9 %copy-start.11 = (f32[32,512]{1,0:T(8,128)}, f32[32,512]{1,0:T(8,128)S(1)}, u32[]{:S(2)}) copy-start(f32[32,512]{1,0:T(8,128)S(1)} %collective-permute-done.8.refs_9_) | copy-start | bytes 196612
  128.3 8.6 %collective-permute-start.11 = (f32[32,512]{1,0:T(8,128)S(1)}, f32[32,512]{1,0:T(8,128)S(1)}, u32[]{:S(2)}, u32[]{:S(2)}) collective-permute-start(f32[32,512]{1,0:T(8,128)S(1)} %collective-permute-done.8.refs_9_), channel_id=1, source_target_pairs={{0,24},{8,0},{16,8},{24,16},{1,25},{9,1},{17,9},{25,17},{2,26},{10... | collective-permute-start | bytes 196616 | tf_op jit(solution)/shard_map/ppermute | solution.py:235
  132.0 5.0 %collective-permute-start.10 = (f32[32,512]{1,0:T(8,128)S(1)}, f32[32,512]{1,0:T(8,128)S(1)}, u32[]{:S(2)}, u32[]{:S(2)}) collective-permute-start(f32[32,512]{1,0:T(8,128)S(1)} %collective-permute-done.8.refs_9_), channel_id=1, source_target_pairs={{0,16},{8,24},{16,0},{24,8},{1,17},{9,25},{17,1},{25,9},{2,18},{10... | collective-permute-start | bytes 196616 | tf_op jit(solution)/shard_map/ppermute | solution.py:235
  134.6 2.6 collective-permute-start.9
  137.0 0.6 copy-start.18
  137.0 0.6 copy-start.22
  137.2 0.6 copy-start.26
  163.8 6.6 %collective-permute-start.12 = (f32[32,512]{1,0:T(8,128)S(1)}, f32[32,512]{1,0:T(8,128)S(1)}, u32[]{:S(2)}, u32[]{:S(2)}) collective-permute-start(f32[32,512]{1,0:T(8,128)S(1)} %reduce_sum.102), channel_id=1, source_target_pairs={{0,0},{1,8},{2,16},{3,24},{4,1},{5,9},{6,17},{7,25},{8,2},{9,10},{... | collective-permute-start | bytes 196616 | tf_op jit(solution)/shard_map/ppermute | solution.py:228
  170.3 8.9 %copy-start.9 = (f32[32,512]{1,0:T(8,128)}, f32[32,512]{1,0:T(8,128)S(1)}, u32[]{:S(2)}) copy-start(f32[32,512]{1,0:T(8,128)S(1)} %collective-permute-done.12.refs_9_) | copy-start | bytes 196612
  170.3 8.6 %collective-permute-start.15 = (f32[32,512]{1,0:T(8,128)S(1)}, f32[32,512]{1,0:T(8,128)S(1)}, u32[]{:S(2)}, u32[]{:S(2)}) collective-permute-start(f32[32,512]{1,0:T(8,128)S(1)} %collective-permute-done.12.refs_9_), channel_id=1, source_target_pairs={{0,24},{8,0},{16,8},{24,16},{1,25},{9,1},{17,9},{25,17},{2,26},{10... | collective-permute-start | bytes 196616 | tf_op jit(solution)/shard_map/ppermute | solution.py:235
  174.0 5.0 %collective-permute-start.14 = (f32[32,512]{1,0:T(8,128)S(1)}, f32[32,512]{1,0:T(8,128)S(1)}, u32[]{:S(2)}, u32[]{:S(2)}) collective-permute-start(f32[32,512]{1,0:T(8,128)S(1)} %collective-permute-done.12.refs_9_), channel_id=1, source_target_pairs={{0,16},{8,24},{16,0},{24,8},{1,17},{9,25},{17,1},{25,9},{2,18},{10... | collective-permute-start | bytes 196616 | tf_op jit(solution)/shard_map/ppermute | solution.py:235
  176.6 2.6 collective-permute-start.13
  179.0 0.6 copy-start.20
  189.8 15.6 %all-to-all-start.4 = ((f32[8,32,512]{2,1,0:T(8,128)}), f32[8,32,512]{2,1,0:T(8,128)}, u32[]{:S(2)}, u32[]{:S(2)}) async-start(f32[8,32,512]{2,1,0:T(8,128)} %bitcast.117), calls=%async_computation.4 | async-start | bytes 1048576 | tf_op jit(solution)/shard_map/all_to_all | solution.py:216
  193.9 2.8 copy-start
  200.1 10.6 %copy-start.4 = (bf16[2,6,64,1024]{3,2,1,0:T(8,128)(2,1)S(1)}, bf16[2,6,64,1024]{3,2,1,0:T(8,128)(2,1)}, u32[]{:S(2)}) copy-start(bf16[2,6,64,1024]{3,2,1,0:T(8,128)(2,1)} %param.11) | copy-start | bytes 4718596
  206.5 45.5 %all-to-all-start.5 = ((f32[8,64,512]{2,1,0:T(8,128)}), f32[8,64,512]{2,1,0:T(8,128)}, u32[]{:S(2)}, u32[]{:S(2)}) async-start(f32[8,64,512]{2,1,0:T(8,128)} %bitcast.8), calls=%async_computation.5 | async-start | bytes 2097152 | tf_op jit(solution)/shard_map/all_to_all | solution.py:216
  210.8 2.4 copy-start.3
  210.9 27.7 %collective-permute-start.16 = (f32[32,512]{1,0:T(8,128)S(1)}, f32[32,512]{1,0:T(8,128)S(1)}, u32[]{:S(2)}, u32[]{:S(2)}) collective-permute-start(f32[32,512]{1,0:T(8,128)S(1)} %reduce_sum.103), channel_id=1, source_target_pairs={{0,0},{1,8},{2,16},{3,24},{4,1},{5,9},{6,17},{7,25},{8,2},{9,10},{... | collective-permute-start | bytes 196616 | tf_op jit(solution)/shard_map/ppermute | solution.py:228
  238.6 4.8 %copy-start.8 = (f32[32,512]{1,0:T(8,128)}, f32[32,512]{1,0:T(8,128)S(1)}, u32[]{:S(2)}) copy-start(f32[32,512]{1,0:T(8,128)S(1)} %collective-permute-done.16.refs_9_) | copy-start | bytes 196612
  238.6 4.3 %collective-permute-start.19 = (f32[32,512]{1,0:T(8,128)S(1)}, f32[32,512]{1,0:T(8,128)S(1)}, u32[]{:S(2)}, u32[]{:S(2)}) collective-permute-start(f32[32,512]{1,0:T(8,128)S(1)} %collective-permute-done.16.refs_9_), channel_id=1, source_target_pairs={{0,24},{8,0},{16,8},{24,16},{1,25},{9,1},{17,9},{25,17},{2,26},{10... | collective-permute-start | bytes 196616 | tf_op jit(solution)/shard_map/ppermute | solution.py:235
  239.3 4.1 %collective-permute-start.18 = (f32[32,512]{1,0:T(8,128)S(1)}, f32[32,512]{1,0:T(8,128)S(1)}, u32[]{:S(2)}, u32[]{:S(2)}) collective-permute-start(f32[32,512]{1,0:T(8,128)S(1)} %collective-permute-done.16.refs_9_), channel_id=1, source_target_pairs={{0,16},{8,24},{16,0},{24,8},{1,17},{9,25},{17,1},{25,9},{2,18},{10... | collective-permute-start | bytes 196616 | tf_op jit(solution)/shard_map/ppermute | solution.py:235
  239.3 4.1 %collective-permute-start.17 = (f32[32,512]{1,0:T(8,128)S(1)}, f32[32,512]{1,0:T(8,128)S(1)}, u32[]{:S(2)}, u32[]{:S(2)}) collective-permute-start(f32[32,512]{1,0:T(8,128)S(1)} %collective-permute-done.16.refs_9_), channel_id=1, source_target_pairs={{0,8},{8,16},{16,24},{24,0},{1,9},{9,17},{17,25},{25,1},{2,10},{10... | collective-permute-start | bytes 196616 | tf_op jit(solution)/shard_map/ppermute | solution.py:235
  242.9 0.6 copy-start.14
  243.4 0.6 copy-start.23
  252.0 10.0 %all-to-all-start.6 = ((f32[8,16,512]{2,1,0:T(8,128)}), f32[8,16,512]{2,1,0:T(8,128)S(1)}, u32[]{:S(2)}, u32[]{:S(2)}) async-start(f32[8,16,512]{2,1,0:T(8,128)} %bitcast.122), calls=%async_computation.6 | async-start | bytes 524288 | tf_op jit(solution)/shard_map/all_to_all | solution.py:216
  259.2 17.0 %copy-start.2 = (bf16[384,2048]{1,0:T(8,128)(2,1)S(1)}, bf16[384,2048]{1,0:T(8,128)(2,1)}, u32[]{:S(2)}) copy-start(bf16[384,2048]{1,0:T(8,128)(2,1)} %get-tuple-element.88.flat_ref) | copy-start | bytes 4718596
  259.2 17.0 %copy-start.6 = (f32[384,384]{1,0:T(8,128)S(1)}, f32[384,384]{1,0:T(8,128)}, u32[]{:S(2)}) copy-start(f32[384,384]{1,0:T(8,128)} %convolution_add_fusion) | copy-start | bytes 1769476
  262.1 7.2 %collective-permute-start.20 = (f32[16,512]{1,0:T(8,128)S(1)}, f32[16,512]{1,0:T(8,128)S(1)}, u32[]{:S(2)}, u32[]{:S(2)}) collective-permute-start(f32[16,512]{1,0:T(8,128)S(1)} %reduce_sum.104), channel_id=1, source_target_pairs={{0,0},{1,8},{2,16},{3,24},{4,1},{5,9},{6,17},{7,25},{8,2},{9,10},{... | collective-permute-start | bytes 98312 | tf_op jit(solution)/shard_map/ppermute | solution.py:228
  269.3 8.6 %copy-start.27 = (f32[16,512]{1,0:T(8,128)}, f32[16,512]{1,0:T(8,128)S(1)}, u32[]{:S(2)}) copy-start(f32[16,512]{1,0:T(8,128)S(1)} %collective-permute-done.20.refs_4_) | copy-start | bytes 98308
  269.3 8.7 %collective-permute-start.23 = (f32[16,512]{1,0:T(8,128)S(1)}, f32[16,512]{1,0:T(8,128)S(1)}, u32[]{:S(2)}, u32[]{:S(2)}) collective-permute-start(f32[16,512]{1,0:T(8,128)S(1)} %collective-permute-done.20.refs_4_), channel_id=1, source_target_pairs={{0,24},{8,0},{16,8},{24,16},{1,25},{9,1},{17,9},{25,17},{2,26},{10... | collective-permute-start | bytes 98312 | tf_op jit(solution)/shard_map/ppermute | solution.py:235
  273.8 4.2 %collective-permute-start.22 = (f32[16,512]{1,0:T(8,128)S(1)}, f32[16,512]{1,0:T(8,128)S(1)}, u32[]{:S(2)}, u32[]{:S(2)}) collective-permute-start(f32[16,512]{1,0:T(8,128)S(1)} %collective-permute-done.20.refs_4_), channel_id=1, source_target_pairs={{0,16},{8,24},{16,0},{24,8},{1,17},{9,25},{17,1},{25,9},{2,18},{10... | collective-permute-start | bytes 98312 | tf_op jit(solution)/shard_map/ppermute | solution.py:235
  276.1 1.9 collective-permute-start.21
  277.9 0.6 copy-start.29
  281.0 2.7 copy-start.1
  281.0 2.8 copy-start.5
  287.4 10.9 %all-to-all-start.7 = ((f32[32,8,128]{2,1,0:T(8,128)}), f32[32,8,128]{2,1,0:T(8,128)S(1)}, u32[]{:S(2)}, u32[]{:S(2)}) async-start(f32[32,8,128]{2,1,0:T(8,128)} %broadcast_in_dim.3), calls=%async_computation.7 | async-start | bytes 262144 | tf_op jit(solution)/shard_map/all_to_all | solution.py:330
  299.7 17.9 %all-to-all-start.8 = ((f32[8,32,512]{2,1,0:T(8,128)}), f32[8,32,512]{2,1,0:T(8,128)S(1)}, u32[]{:S(2)}, u32[]{:S(2)}) async-start(f32[8,32,512]{2,1,0:T(8,128)} %bitcast.19), calls=%async_computation.8 | async-start | bytes 1048576 | tf_op jit(solution)/shard_map/all_to_all | solution.py:216
  317.7 13.5 %collective-permute-start.24 = (f32[96,512]{1,0:T(8,128)S(1)}, f32[96,512]{1,0:T(8,128)S(1)}, u32[]{:S(2)}, u32[]{:S(2)}) collective-permute-start(f32[96,512]{1,0:T(8,128)S(1)} %pad_maximum_fusion.3), channel_id=1, source_target_pairs={{0,0},{1,8},{2,16},{3,24},{4,1},{5,9},{6,17},{7,25},{8,2},{9,10},{... | collective-permute-start | bytes 589832 | tf_op jit(solution)/shard_map/ppermute | solution.py:228
  331.2 15.8 %collective-permute-start.27 = (f32[96,512]{1,0:T(8,128)S(1)}, f32[96,512]{1,0:T(8,128)S(1)}, u32[]{:S(2)}, u32[]{:S(2)}) collective-permute-start(f32[96,512]{1,0:T(8,128)S(1)} %collective-permute-done.24), channel_id=1, source_target_pairs={{0,24},{8,0},{16,8},{24,16},{1,25},{9,1},{17,9},{25,17},{2,26},{10... | collective-permute-start | bytes 589832 | tf_op jit(solution)/shard_map/ppermute | solution.py:235
  333.2 13.8 %collective-permute-start.26 = (f32[96,512]{1,0:T(8,128)S(1)}, f32[96,512]{1,0:T(8,128)S(1)}, u32[]{:S(2)}, u32[]{:S(2)}) collective-permute-start(f32[96,512]{1,0:T(8,128)S(1)} %collective-permute-done.24), channel_id=1, source_target_pairs={{0,16},{8,24},{16,0},{24,8},{1,17},{9,25},{17,1},{25,9},{2,18},{10... | collective-permute-start | bytes 589832 | tf_op jit(solution)/shard_map/ppermute | solution.py:235
  333.2 13.8 %collective-permute-start.25 = (f32[96,512]{1,0:T(8,128)S(1)}, f32[96,512]{1,0:T(8,128)S(1)}, u32[]{:S(2)}, u32[]{:S(2)}) collective-permute-start(f32[96,512]{1,0:T(8,128)S(1)} %collective-permute-done.24), channel_id=1, source_target_pairs={{0,8},{8,16},{16,24},{24,0},{1,9},{9,17},{17,25},{25,1},{2,10},{10... | collective-permute-start | bytes 589832 | tf_op jit(solution)/shard_map/ppermute | solution.py:235
  347.3 0.9 copy-start.31
  (7 other events, 4.3 us)

commit v3 on v2

--- a/solution.py
+++ b/solution.py
@@ -10,7 +10,7 @@
 NT = (((1,), (1,)), ((), ()))
 TN = (((0,), (0,)), ((), ()))
 VMEM_LIMIT = 60 * 1024 * 1024
-CUT = 2
+CUT = 3
 
 
 def step_kernel(plan, products, parts, *refs):

time: 350 us -> 354 us (1.011)
  waiting for transfers between devices: 96.3 us -> 117 us
  blocking collectives: 31.8 us -> 16.8 us
    all_to_all x6 -> x7, waiting for transfers between devices: 23.3 us -> 46.8 us  [swap(): return lax.all_to_all(pieces, 'col', 0, 0, tiled=True)]
    all_to_all x2 -> x1, blocking collectives: 31.8 us -> 16.8 us  [swap(): return lax.all_to_all(pieces, 'col', 0, 0, tiled=True)]
    ppermute x7, waiting for transfers between devices: 56.8 us -> 49.9 us  [place(): return lax.ppermute(mine, ('row', 'col'), moves)]
    ppermute x21, waiting for transfers between devices: 12.3 us -> 16.1 us  [gather(): lax.ppermute(mine, 'row', [(i, (i + s) % rows) for i in range(rows)])]
    all_to_all x6 -> x7, starting transfers between devices: 25.9 us -> 28.3 us  [swap(): return lax.all_to_all(pieces, 'col', 0, 0, tiled=True)]
    unnamed x75 -> x77, local copies, waits for them, and re-layouts: 18.2 us -> 18.3 us
  transfers between devices with their start and end apart: 35 -> 36, of which waited for: 23 -> 27; matrix products, arithmetic and copies ran while one was open for 7% -> 7% of each run, Pallas kernels for 9% -> 10%
where the time goes in v3:
time: 354 us; the launch traced here: 352 us
  waiting for transfers between devices  117 us (33%)
  Pallas kernels  81.5 us (23%)
  starting transfers between devices  81.4 us (23%)
  local copies, waits for them, and re-layouts  30.9 us (9%)
  matrix products  18.6 us (5%)
  blocking collectives  16.8 us (5%)
    pallas_call x7, Pallas kernels, run_step(): pl.pallas_call(functools.partial(step_kernel, plan, [[which for which, _...  57.2 us
    ppermute x7, waiting for transfers between devices, place(): return lax.ppermute(mine, ('row', 'col'), moves)  49.9 us
    all_to_all x7, waiting for transfers between devices, swap(): return lax.all_to_all(pieces, 'col', 0, 0, tiled=True)  46.8 us
    ppermute x21, starting transfers between devices, gather(): lax.ppermute(mine, 'row', [(i, (i + s) % rows) for i in range(rows)])  34.9 us
    all_to_all x7, starting transfers between devices, swap(): return lax.all_to_all(pieces, 'col', 0, 0, tiled=True)  28.3 us
    pallas_call x2, Pallas kernels, layer_grads(): pl.pallas_call(grads_kernel_keep if before else grads_kernel, grid=(rows...  24.3 us
    unnamed x77, local copies, waits for them, and re-layouts  18.3 us
    all_to_all x1, blocking collectives, swap(): return lax.all_to_all(pieces, 'col', 0, 0, tiled=True)  16.8 us
  transfers between devices with their start and end apart: 36, of which 27 were waited for; matrix products, arithmetic and copies ran while one was open for 7% of the time, Pallas kernels for 10%

profile of v3, /device:TPU:5, one launch (start us, length us, event | category | flops | bytes accessed | tf_op | source)
XLA Modules:
  0.0 352.0 jit_solution(9589094695422205045)
XLA Ops:
  0.6 2.2 slice-done
  2.8 3.4 copy.25
  6.2 2.2 slice-done.2
  8.4 3.4 copy.24
  11.8 6.9 %shard_map.94 = (bf16[384,2048]{1,0:T(8,128)(2,1)}, f32[64,512]{1,0:T(8,128)}, f32[2,128,512]{2,1,0:T(8,128)}) custom-call(f32[2,6,64,4,512]{4,3,2,1,0:T(4,128)} %refs_0_.13, f32[2,7,64,512]{3,2,1,0:T(8,128)} %refs_2_.13, f32[2,7,64,512]{3,2,1,0:T(8,128)} %refs_2_.13, f32[6,64,512]{2,1,0:T(8,128)} %refs_4_.9, bf16[1024,2048]{1,0:T(8,128)(2,1)} %bitcast.96, ...), custom_call_target="tpu_custom_call" | custom-call | flops 536871936 | bytes 9388608 | tf_op jit(solution)/shard_map/pallas_call | solution.py:137
  18.7 5.8 %all-to-all-start = ((f32[8,32,512]{2,1,0:T(8,128)}), f32[8,32,512]{2,1,0:T(8,128)S(1)}, u32[]{:S(2)}, u32[]{:S(2)}) async-start(f32[8,32,512]{2,1,0:T(8,128)} %bitcast.121), calls=%async_computation | async-start | bytes 1048576 | tf_op jit(solution)/shard_map/all_to_all | solution.py:216
  24.4 2.2 slice-done.3
  26.6 3.4 copy.26
  30.0 8.2 %all-to-all-done = f32[8,32,512]{2,1,0:T(8,128)S(1)} async-done(((f32[8,32,512]{2,1,0:T(8,128)}), f32[8,32,512]{2,1,0:T(8,128)S(1)}, u32[]{:S(2)}, u32[]{:S(2)}) %all-to-all-start) | async-done | bytes 524320 | tf_op jit(solution)/shard_map/all_to_all | solution.py:216
  38.2 1.9 collective-permute-start
  40.2 4.7 %collective-permute-done.refs_8_ = f32[32,512]{1,0:T(8,128)S(1)} collective-permute-done((f32[32,512]{1,0:T(8,128)S(1)}, f32[32,512]{1,0:T(8,128)S(1)}, u32[]{:S(2)}, u32[]{:S(2)}) %collective-permute-start) | collective-permute-done | bytes 65568 | tf_op jit(solution)/shard_map/ppermute | solution.py:228
  44.9 5.6 %collective-permute-start.1 = (f32[32,512]{1,0:T(8,128)S(1)}, f32[32,512]{1,0:T(8,128)S(1)}, u32[]{:S(2)}, u32[]{:S(2)}) collective-permute-start(f32[32,512]{1,0:T(8,128)S(1)} %collective-permute-done.refs_8_), channel_id=1, source_target_pairs={{0,8},{8,16},{16,24},{24,0},{1,9},{9,17},{17,25},{25,1},{2,10},{10... | collective-permute-start | bytes 196616 | tf_op jit(solution)/shard_map/ppermute | solution.py:235
  51.8 1.9 collective-permute-done.2.refs_10_
  55.0 9.9 %shard_map.95 = (bf16[384,2048]{1,0:T(8,128)(2,1)}, f32[64,512]{1,0:T(8,128)}, bf16[384,2048]{1,0:T(8,128)(2,1)}, f32[64,512]{1,0:T(8,128)}, f32[2,128,512]{2,1,0:T(8,128)}) custom-call(f32[2,6,64,4,512]{4,3,2,1,0:T(4,128)} %refs_0_.13, f32[2,7,64,512]{3,2,1,0:T(8,128)} %refs_2_.13, f32[2,7,64,512]{3,2,1,0:T(8,128)} %refs_2_.13, ...), custom_call_target="tpu_custom_call", output_to_operand_aliasing={{0}: (16, {})} | custom-call | flops 805307392 | bytes 13582912 | tf_op jit(solution)/shard_map/pallas_call | solution.py:137
  64.8 3.5 all-to-all-start.1
  68.3 2.2 slice-done.1
  70.5 3.4 copy.27
  73.9 7.8 %all-to-all-done.1 = f32[8,32,512]{2,1,0:T(8,128)S(1)} async-done(((f32[8,32,512]{2,1,0:T(8,128)}), f32[8,32,512]{2,1,0:T(8,128)S(1)}, u32[]{:S(2)}, u32[]{:S(2)}) %all-to-all-start.1) | async-done | bytes 524320 | tf_op jit(solution)/shard_map/all_to_all | solution.py:216
  81.7 1.9 collective-permute-start.4
  83.6 4.6 %collective-permute-done.4.refs_9_ = f32[32,512]{1,0:T(8,128)S(1)} collective-permute-done((f32[32,512]{1,0:T(8,128)S(1)}, f32[32,512]{1,0:T(8,128)S(1)}, u32[]{:S(2)}, u32[]{:S(2)}) %collective-permute-start.4) | collective-permute-done | bytes 65568 | tf_op jit(solution)/shard_map/ppermute | solution.py:228
  88.2 5.6 %collective-permute-start.5 = (f32[32,512]{1,0:T(8,128)S(1)}, f32[32,512]{1,0:T(8,128)S(1)}, u32[]{:S(2)}, u32[]{:S(2)}) collective-permute-start(f32[32,512]{1,0:T(8,128)S(1)} %collective-permute-done.4.refs_9_), channel_id=1, source_target_pairs={{0,8},{8,16},{16,24},{24,0},{1,9},{9,17},{17,25},{25,1},{2,10},{10... | collective-permute-start | bytes 196616 | tf_op jit(solution)/shard_map/ppermute | solution.py:235
  95.2 1.9 collective-permute-done.6.refs_11_
  98.3 10.0 %shard_map.96 = (bf16[384,2048]{1,0:T(8,128)(2,1)}, f32[64,512]{1,0:T(8,128)}, bf16[384,2048]{1,0:T(8,128)(2,1)}, f32[64,512]{1,0:T(8,128)}, f32[2,128,512]{2,1,0:T(8,128)}) custom-call(f32[2,6,64,4,512]{4,3,2,1,0:T(4,128)} %refs_0_.13, f32[2,7,64,512]{3,2,1,0:T(8,128)} %refs_2_.13, ...), custom_call_target="tpu_custom_call", output_to_operand_aliasing={{0}: (17, {}), {2}: (18, {})} | custom-call | flops 805307392 | bytes 13582912 | tf_op jit(solution)/shard_map/pallas_call | solution.py:137
  108.3 16.8 %all_to_all.45 = f32[8,32,512]{2,1,0:T(8,128)S(1)} all-to-all(f32[8,32,512]{2,1,0:T(8,128)} %bitcast.120), channel_id=1, replica_groups=mesh['row'=4,'col'=8] {'col'}, dimensions={0} | all-to-all | bytes 1048576 | tf_op jit(solution)/shard_map/all_to_all | solution.py:216
  125.1 2.1 collective-permute-start.8
  127.2 4.4 %collective-permute-done.8.refs_9_ = f32[32,512]{1,0:T(8,128)S(1)} collective-permute-done((f32[32,512]{1,0:T(8,128)S(1)}, f32[32,512]{1,0:T(8,128)S(1)}, u32[]{:S(2)}, u32[]{:S(2)}) %collective-permute-start.8) | collective-permute-done | bytes 65568 | tf_op jit(solution)/shard_map/ppermute | solution.py:228
  131.6 3.2 collective-permute-start.10
  134.9 2.8 collective-permute-start.11
  137.7 2.2 collective-permute-done.11.refs_12_
  140.6 10.0 %shard_map.97 = (bf16[384,2048]{1,0:T(8,128)(2,1)}, f32[64,512]{1,0:T(8,128)}, bf16[384,2048]{1,0:T(8,128)(2,1)}, f32[64,512]{1,0:T(8,128)}, f32[2,128,512]{2,1,0:T(8,128)}) custom-call(f32[2,6,64,4,512]{4,3,2,1,0:T(4,128)} %refs_0_.13, f32[2,7,64,512]{3,2,1,0:T(8,128)} %refs_2_.13, ...), custom_call_target="tpu_custom_call", output_to_operand_aliasing={{0}: (17, {}), {2}: (18, {})} | custom-call | flops 805307392 | bytes 13582912 | tf_op jit(solution)/shard_map/pallas_call | solution.py:137
  150.6 3.4 all-to-all-start.3
  154.0 2.8 fusion.8
  156.8 2.4 fusion.14
  160.2 7.5 %all-to-all-done.3 = f32[8,32,512]{2,1,0:T(8,128)S(1)} async-done(((f32[8,32,512]{2,1,0:T(8,128)}), f32[8,32,512]{2,1,0:T(8,128)S(1)}, u32[]{:S(2)}, u32[]{:S(2)}) %all-to-all-start.3) | async-done | bytes 524320 | tf_op jit(solution)/shard_map/all_to_all | solution.py:216
  167.8 4.6 %all-to-all-start.4 = ((f32[8,48,512]{2,1,0:T(8,128)}), f32[8,48,512]{2,1,0:T(8,128)S(1)}, u32[]{:S(2)}, u32[]{:S(2)}) async-start(f32[8,48,512]{2,1,0:T(8,128)} %bitcast.7), calls=%async_computation.4 | async-start | bytes 1572864 | tf_op jit(solution)/shard_map/all_to_all | solution.py:216
  172.3 3.1 collective-permute-start.12
  175.4 20.1 %collective-permute-done.12.refs_9_ = f32[32,512]{1,0:T(8,128)S(1)} collective-permute-done((f32[32,512]{1,0:T(8,128)S(1)}, f32[32,512]{1,0:T(8,128)S(1)}, u32[]{:S(2)}, u32[]{:S(2)}) %collective-permute-start.12) | collective-permute-done | bytes 65568 | tf_op jit(solution)/shard_map/ppermute | solution.py:228
  195.5 1.8 collective-permute-start.14
  197.4 3.2 collective-permute-done.14.refs_11_
  201.8 10.0 %shard_map.98 = (bf16[384,2048]{1,0:T(8,128)(2,1)}, f32[64,512]{1,0:T(8,128)}, bf16[384,2048]{1,0:T(8,128)(2,1)}, f32[64,512]{1,0:T(8,128)}, f32[2,128,512]{2,1,0:T(8,128)}) custom-call(f32[2,6,64,4,512]{4,3,2,1,0:T(4,128)} %refs_0_.13, f32[2,7,64,512]{3,2,1,0:T(8,128)} %refs_2_.13, ...), custom_call_target="tpu_custom_call", output_to_operand_aliasing={{0}: (17, {}), {2}: (18, {})} | custom-call | flops 805307392 | bytes 13582912 | tf_op jit(solution)/shard_map/pallas_call | solution.py:137
  211.8 3.5 all-to-all-start.5
  216.8 11.8 %all-to-all-done.5 = f32[8,32,512]{2,1,0:T(8,128)S(1)} async-done(((f32[8,32,512]{2,1,0:T(8,128)}), f32[8,32,512]{2,1,0:T(8,128)S(1)}, u32[]{:S(2)}, u32[]{:S(2)}) %all-to-all-start.5) | async-done | bytes 524320 | tf_op jit(solution)/shard_map/all_to_all | solution.py:216
  228.7 1.9 collective-permute-start.16
  232.2 3.0 collective-permute-done.16.refs_9_
  235.2 4.7 %collective-permute-start.17 = (f32[32,512]{1,0:T(8,128)S(1)}, f32[32,512]{1,0:T(8,128)S(1)}, u32[]{:S(2)}, u32[]{:S(2)}) collective-permute-start(f32[32,512]{1,0:T(8,128)S(1)} %collective-permute-done.16.refs_9_), channel_id=1, source_target_pairs={{0,8},{8,16},{16,24},{24,0},{1,9},{9,17},{17,25},{25,1},{2,10},{10... | collective-permute-start | bytes 196616 | tf_op jit(solution)/shard_map/ppermute | solution.py:235
  244.3 8.0 %shard_map.99 = (bf16[384,2048]{1,0:T(8,128)(2,1)}, bf16[384,2048]{1,0:T(8,128)(2,1)}, f32[64,512]{1,0:T(8,128)}, f32[2,64,512]{2,1,0:T(8,128)}) custom-call(f32[2,6,64,4,512]{4,3,2,1,0:T(4,128)} %refs_0_.13, f32[2,7,64,512]{3,2,1,0:T(8,128)} %refs_2_.13, f32[2,7,64,512]{3,2,1,0:T(8,128)} %refs_2_.13, ...), custom_call_target="tpu_custom_call", output_to_operand_aliasing={{0}: (16, {}), {1}: (17, {})} | custom-call | flops 536871936 | bytes 9388608 | tf_op jit(solution)/shard_map/pallas_call | solution.py:137
  252.3 3.5 all-to-all-start.6
  258.7 4.1 %all-to-all-done.6 = f32[8,16,512]{2,1,0:T(8,128)S(1)} async-done(((f32[8,16,512]{2,1,0:T(8,128)}), f32[8,16,512]{2,1,0:T(8,128)S(1)}, u32[]{:S(2)}, u32[]{:S(2)}) %all-to-all-start.6) | async-done | bytes 262176 | tf_op jit(solution)/shard_map/all_to_all | solution.py:216
  262.8 2.4 collective-permute-start.20
  265.9 3.1 collective-permute-done.20.refs_4_
  269.0 6.5 %collective-permute-start.21 = (f32[16,512]{1,0:T(8,128)S(1)}, f32[16,512]{1,0:T(8,128)S(1)}, u32[]{:S(2)}, u32[]{:S(2)}) collective-permute-start(f32[16,512]{1,0:T(8,128)S(1)} %collective-permute-done.20.refs_4_), channel_id=1, source_target_pairs={{0,8},{8,16},{16,24},{24,0},{1,9},{9,17},{17,25},{25,1},{2,10},{10... | collective-permute-start | bytes 98312 | tf_op jit(solution)/shard_map/ppermute | solution.py:235
  275.9 1.7 fusion.25
  279.4 2.5 shard_map.100.flat_ref
  281.9 2.8 fusion.11
  288.3 3.0 all-to-all-start.7
  291.4 2.4 fusion.17
  294.8 3.8 %all-to-all-done.7 = f32[32,8,128]{2,1,0:T(8,128)S(1)} async-done(((f32[32,8,128]{2,1,0:T(8,128)}), f32[32,8,128]{2,1,0:T(8,128)S(1)}, u32[]{:S(2)}, u32[]{:S(2)}) %all-to-all-start.7) | async-done | bytes 131104 | tf_op jit(solution)/shard_map/all_to_all | solution.py:330
  299.9 4.1 %all-to-all-start.8 = ((f32[8,48,512]{2,1,0:T(8,128)}), f32[8,48,512]{2,1,0:T(8,128)S(1)}, u32[]{:S(2)}, u32[]{:S(2)}) async-start(f32[8,48,512]{2,1,0:T(8,128)} %bitcast.19), calls=%async_computation.8 | async-start | bytes 1572864 | tf_op jit(solution)/shard_map/all_to_all | solution.py:216
  304.1 12.2 %shard_map.101 = (bf16[2,1024,4,512]{3,2,1,0:T(4,128)(2,1)}, bf16[2,1024,4,512]{3,2,1,0:T(4,128)(2,1)}) custom-call(f32[1,1]{1,0:T(1,128)} %bitcast.16.scale_ref, bf16[2,384,1024]{2,1,0:T(8,128)(2,1)} %bitcast.109, bf16[2,384,1024]{2,1,0:T(8,128)(2,1)} %bitcast.111, bf16[384,2048]{1,0:T(8,128)(2,1)} %get-tuple-element.92.flat_ref), custom_call_target="tpu_custom_call" | custom-call | flops 3221225472 | bytes 8388608 | tf_op jit(solution)/shard_map/pallas_call | solution.py:189
  316.2 7.3 %all-to-all-done.8 = f32[8,48,512]{2,1,0:T(8,128)S(1)} async-done(((f32[8,48,512]{2,1,0:T(8,128)}), f32[8,48,512]{2,1,0:T(8,128)S(1)}, u32[]{:S(2)}, u32[]{:S(2)}) %all-to-all-start.8) | async-done | bytes 786464 | tf_op jit(solution)/shard_map/all_to_all | solution.py:216
  323.6 1.9 collective-permute-start.24
  325.6 10.0 %collective-permute-done.24 = f32[96,512]{1,0:T(8,128)S(1)} collective-permute-done((f32[96,512]{1,0:T(8,128)S(1)}, f32[96,512]{1,0:T(8,128)S(1)}, u32[]{:S(2)}, u32[]{:S(2)}) %collective-permute-start.24) | collective-permute-done | bytes 196640 | tf_op jit(solution)/shard_map/ppermute | solution.py:228
  336.3 2.3 collective-permute-start.26
  338.6 12.2 %shard_map.102 = (bf16[2,1024,4,512]{3,2,1,0:T(4,128)(2,1)}, bf16[2,1024,4,512]{3,2,1,0:T(4,128)(2,1)}) custom-call(f32[1,1]{1,0:T(1,128)} %bitcast.16.scale_ref, bf16[2,384,1024]{2,1,0:T(8,128)(2,1)} %bitcast.110, bf16[2,384,1024]{2,1,0:T(8,128)(2,1)} %bitcast.112, ...), custom_call_target="tpu_custom_call", output_to_operand_aliasing={{0}: (4, {}), {1}: (5, {})} | custom-call | flops 3221225472 | bytes 8388608 | tf_op jit(solution)/shard_map/pallas_call | solution.py:189
  (130 shorter events, 27.2 us)
Async XLA Ops:
  0.6 2.2 slice-start
  6.2 2.2 slice-start.2
  18.7 19.5 %all-to-all-start = ((f32[8,32,512]{2,1,0:T(8,128)}), f32[8,32,512]{2,1,0:T(8,128)S(1)}, u32[]{:S(2)}, u32[]{:S(2)}) async-start(f32[8,32,512]{2,1,0:T(8,128)} %bitcast.121), calls=%async_computation | async-start | bytes 1048576 | tf_op jit(solution)/shard_map/all_to_all | solution.py:216
  24.4 2.2 slice-start.3
  38.2 6.6 %collective-permute-start = (f32[32,512]{1,0:T(8,128)S(1)}, f32[32,512]{1,0:T(8,128)S(1)}, u32[]{:S(2)}, u32[]{:S(2)}) collective-permute-start(f32[32,512]{1,0:T(8,128)S(1)} %reduce_sum.99), channel_id=1, source_target_pairs={{0,0},{1,8},{2,16},{3,24},{4,1},{5,9},{6,17},{7,25},{8,2},{9,10},{... | collective-permute-start | bytes 196616 | tf_op jit(solution)/shard_map/ppermute | solution.py:228
  44.9 9.4 %copy-start.8 = (f32[32,512]{1,0:T(8,128)}, f32[32,512]{1,0:T(8,128)S(1)}, u32[]{:S(2)}) copy-start(f32[32,512]{1,0:T(8,128)S(1)} %collective-permute-done.refs_8_) | copy-start | bytes 196612
  44.9 7.0 %collective-permute-start.1 = (f32[32,512]{1,0:T(8,128)S(1)}, f32[32,512]{1,0:T(8,128)S(1)}, u32[]{:S(2)}, u32[]{:S(2)}) collective-permute-start(f32[32,512]{1,0:T(8,128)S(1)} %collective-permute-done.refs_8_), channel_id=1, source_target_pairs={{0,8},{8,16},{16,24},{24,0},{1,9},{9,17},{17,25},{25,1},{2,10},{10... | collective-permute-start | bytes 196616 | tf_op jit(solution)/shard_map/ppermute | solution.py:235
  50.5 3.2 collective-permute-start.2
  50.5 3.8 %collective-permute-start.3 = (f32[32,512]{1,0:T(8,128)S(1)}, f32[32,512]{1,0:T(8,128)S(1)}, u32[]{:S(2)}, u32[]{:S(2)}) collective-permute-start(f32[32,512]{1,0:T(8,128)S(1)} %collective-permute-done.refs_8_), channel_id=1, source_target_pairs={{0,24},{8,0},{16,8},{24,16},{1,25},{9,1},{17,9},{25,17},{2,26},{10... | collective-permute-start | bytes 196616 | tf_op jit(solution)/shard_map/ppermute | solution.py:235
  51.8 2.5 copy-start.13
  64.8 16.8 %all-to-all-start.1 = ((f32[8,32,512]{2,1,0:T(8,128)}), f32[8,32,512]{2,1,0:T(8,128)S(1)}, u32[]{:S(2)}, u32[]{:S(2)}) async-start(f32[8,32,512]{2,1,0:T(8,128)} %bitcast.119), calls=%async_computation.1 | async-start | bytes 1048576 | tf_op jit(solution)/shard_map/all_to_all | solution.py:216
  68.3 2.2 slice-start.1
  81.7 6.5 %collective-permute-start.4 = (f32[32,512]{1,0:T(8,128)S(1)}, f32[32,512]{1,0:T(8,128)S(1)}, u32[]{:S(2)}, u32[]{:S(2)}) collective-permute-start(f32[32,512]{1,0:T(8,128)S(1)} %reduce_sum.100), channel_id=1, source_target_pairs={{0,0},{1,8},{2,16},{3,24},{4,1},{5,9},{6,17},{7,25},{8,2},{9,10},{... | collective-permute-start | bytes 196616 | tf_op jit(solution)/shard_map/ppermute | solution.py:228
  88.2 9.4 %copy-start.11 = (f32[32,512]{1,0:T(8,128)}, f32[32,512]{1,0:T(8,128)S(1)}, u32[]{:S(2)}) copy-start(f32[32,512]{1,0:T(8,128)S(1)} %collective-permute-done.4.refs_9_) | copy-start | bytes 196612
  88.2 6.9 %collective-permute-start.5 = (f32[32,512]{1,0:T(8,128)S(1)}, f32[32,512]{1,0:T(8,128)S(1)}, u32[]{:S(2)}, u32[]{:S(2)}) collective-permute-start(f32[32,512]{1,0:T(8,128)S(1)} %collective-permute-done.4.refs_9_), channel_id=1, source_target_pairs={{0,8},{8,16},{16,24},{24,0},{1,9},{9,17},{17,25},{25,1},{2,10},{10... | collective-permute-start | bytes 196616 | tf_op jit(solution)/shard_map/ppermute | solution.py:235
  93.8 3.2 collective-permute-start.6
  93.8 3.8 %collective-permute-start.7 = (f32[32,512]{1,0:T(8,128)S(1)}, f32[32,512]{1,0:T(8,128)S(1)}, u32[]{:S(2)}, u32[]{:S(2)}) collective-permute-start(f32[32,512]{1,0:T(8,128)S(1)} %collective-permute-done.4.refs_9_), channel_id=1, source_target_pairs={{0,24},{8,0},{16,8},{24,16},{1,25},{9,1},{17,9},{25,17},{2,26},{10... | collective-permute-start | bytes 196616 | tf_op jit(solution)/shard_map/ppermute | solution.py:235
  95.2 2.5 copy-start.18
  125.1 6.5 %collective-permute-start.8 = (f32[32,512]{1,0:T(8,128)S(1)}, f32[32,512]{1,0:T(8,128)S(1)}, u32[]{:S(2)}, u32[]{:S(2)}) collective-permute-start(f32[32,512]{1,0:T(8,128)S(1)} %reduce_sum.101), channel_id=1, source_target_pairs={{0,0},{1,8},{2,16},{3,24},{4,1},{5,9},{6,17},{7,25},{8,2},{9,10},{... | collective-permute-start | bytes 196616 | tf_op jit(solution)/shard_map/ppermute | solution.py:228
  131.6 8.3 %copy-start.12 = (f32[32,512]{1,0:T(8,128)}, f32[32,512]{1,0:T(8,128)S(1)}, u32[]{:S(2)}) copy-start(f32[32,512]{1,0:T(8,128)S(1)} %collective-permute-done.8.refs_9_) | copy-start | bytes 196612
  131.6 6.0 %collective-permute-start.10 = (f32[32,512]{1,0:T(8,128)S(1)}, f32[32,512]{1,0:T(8,128)S(1)}, u32[]{:S(2)}, u32[]{:S(2)}) collective-permute-start(f32[32,512]{1,0:T(8,128)S(1)} %collective-permute-done.8.refs_9_), channel_id=1, source_target_pairs={{0,16},{8,24},{16,0},{24,8},{1,17},{9,25},{17,1},{25,9},{2,18},{10... | collective-permute-start | bytes 196616 | tf_op jit(solution)/shard_map/ppermute | solution.py:235
  134.9 5.0 %collective-permute-start.11 = (f32[32,512]{1,0:T(8,128)S(1)}, f32[32,512]{1,0:T(8,128)S(1)}, u32[]{:S(2)}, u32[]{:S(2)}) collective-permute-start(f32[32,512]{1,0:T(8,128)S(1)} %collective-permute-done.8.refs_9_), channel_id=1, source_target_pairs={{0,24},{8,0},{16,8},{24,16},{1,25},{9,1},{17,9},{25,17},{2,26},{10... | collective-permute-start | bytes 196616 | tf_op jit(solution)/shard_map/ppermute | solution.py:235
  137.6 2.3 collective-permute-start.9
  137.7 2.3 copy-start.19
  139.9 0.7 copy-start.27
  150.6 17.2 %all-to-all-start.3 = ((f32[8,32,512]{2,1,0:T(8,128)}), f32[8,32,512]{2,1,0:T(8,128)S(1)}, u32[]{:S(2)}, u32[]{:S(2)}) async-start(f32[8,32,512]{2,1,0:T(8,128)} %bitcast.118), calls=%async_computation.3 | async-start | bytes 1048576 | tf_op jit(solution)/shard_map/all_to_all | solution.py:216
  154.0 2.8 copy-start
  167.8 44.0 %all-to-all-start.4 = ((f32[8,48,512]{2,1,0:T(8,128)}), f32[8,48,512]{2,1,0:T(8,128)S(1)}, u32[]{:S(2)}, u32[]{:S(2)}) async-start(f32[8,48,512]{2,1,0:T(8,128)} %bitcast.7), calls=%async_computation.4 | async-start | bytes 1572864 | tf_op jit(solution)/shard_map/all_to_all | solution.py:216
  172.3 23.2 %collective-permute-start.12 = (f32[32,512]{1,0:T(8,128)S(1)}, f32[32,512]{1,0:T(8,128)S(1)}, u32[]{:S(2)}, u32[]{:S(2)}) collective-permute-start(f32[32,512]{1,0:T(8,128)S(1)} %reduce_sum.102), channel_id=1, source_target_pairs={{0,0},{1,8},{2,16},{3,24},{4,1},{5,9},{6,17},{7,25},{8,2},{9,10},{... | collective-permute-start | bytes 196616 | tf_op jit(solution)/shard_map/ppermute | solution.py:228
  195.5 5.6 %copy-start.10 = (f32[32,512]{1,0:T(8,128)}, f32[32,512]{1,0:T(8,128)S(1)}, u32[]{:S(2)}) copy-start(f32[32,512]{1,0:T(8,128)S(1)} %collective-permute-done.12.refs_9_) | copy-start | bytes 196612
  195.5 1.8 collective-permute-start.13
  195.5 5.1 %collective-permute-start.14 = (f32[32,512]{1,0:T(8,128)S(1)}, f32[32,512]{1,0:T(8,128)S(1)}, u32[]{:S(2)}, u32[]{:S(2)}) collective-permute-start(f32[32,512]{1,0:T(8,128)S(1)} %collective-permute-done.12.refs_9_), channel_id=1, source_target_pairs={{0,16},{8,24},{16,0},{24,8},{1,17},{9,25},{17,1},{25,9},{2,18},{10... | collective-permute-start | bytes 196616 | tf_op jit(solution)/shard_map/ppermute | solution.py:235
  197.4 3.8 %collective-permute-start.15 = (f32[32,512]{1,0:T(8,128)S(1)}, f32[32,512]{1,0:T(8,128)S(1)}, u32[]{:S(2)}, u32[]{:S(2)}) collective-permute-start(f32[32,512]{1,0:T(8,128)S(1)} %collective-permute-done.12.refs_9_), channel_id=1, source_target_pairs={{0,24},{8,0},{16,8},{24,16},{1,25},{9,1},{17,9},{25,17},{2,26},{10... | collective-permute-start | bytes 196616 | tf_op jit(solution)/shard_map/ppermute | solution.py:235
  197.4 3.8 %copy-start.16 = (f32[32,512]{1,0:T(8,128)}, f32[32,512]{1,0:T(8,128)S(1)}, u32[]{:S(2)}) copy-start(f32[32,512]{1,0:T(8,128)S(1)} %collective-permute-done.13.refs_10_) | copy-start | bytes 196612
  201.1 0.6 copy-start.25
  211.8 5.1 %copy-start.3 = (f32[8,48,512]{2,1,0:T(8,128)}, f32[8,48,512]{2,1,0:T(8,128)S(1)}, u32[]{:S(2)}) copy-start(f32[8,48,512]{2,1,0:T(8,128)S(1)} %all-to-all-done.4) | copy-start | bytes 2359300
  211.8 16.9 %all-to-all-start.5 = ((f32[8,32,512]{2,1,0:T(8,128)}), f32[8,32,512]{2,1,0:T(8,128)S(1)}, u32[]{:S(2)}, u32[]{:S(2)}) async-start(f32[8,32,512]{2,1,0:T(8,128)} %bitcast.117), calls=%async_computation.5 | async-start | bytes 1048576 | tf_op jit(solution)/shard_map/all_to_all | solution.py:216
  228.7 6.5 %collective-permute-start.16 = (f32[32,512]{1,0:T(8,128)S(1)}, f32[32,512]{1,0:T(8,128)S(1)}, u32[]{:S(2)}, u32[]{:S(2)}) collective-permute-start(f32[32,512]{1,0:T(8,128)S(1)} %reduce_sum.103), channel_id=1, source_target_pairs={{0,0},{1,8},{2,16},{3,24},{4,1},{5,9},{6,17},{7,25},{8,2},{9,10},{... | collective-permute-start | bytes 196616 | tf_op jit(solution)/shard_map/ppermute | solution.py:228
  235.2 8.5 %copy-start.9 = (f32[32,512]{1,0:T(8,128)}, f32[32,512]{1,0:T(8,128)S(1)}, u32[]{:S(2)}) copy-start(f32[32,512]{1,0:T(8,128)S(1)} %collective-permute-done.16.refs_9_) | copy-start | bytes 196612
  235.2 6.5 %collective-permute-start.17 = (f32[32,512]{1,0:T(8,128)S(1)}, f32[32,512]{1,0:T(8,128)S(1)}, u32[]{:S(2)}, u32[]{:S(2)}) collective-permute-start(f32[32,512]{1,0:T(8,128)S(1)} %collective-permute-done.16.refs_9_), channel_id=1, source_target_pairs={{0,8},{8,16},{16,24},{24,0},{1,9},{9,17},{17,25},{25,1},{2,10},{10... | collective-permute-start | bytes 196616 | tf_op jit(solution)/shard_map/ppermute | solution.py:235
  239.9 3.2 collective-permute-start.18
  239.9 3.8 %collective-permute-start.19 = (f32[32,512]{1,0:T(8,128)S(1)}, f32[32,512]{1,0:T(8,128)S(1)}, u32[]{:S(2)}, u32[]{:S(2)}) collective-permute-start(f32[32,512]{1,0:T(8,128)S(1)} %collective-permute-done.16.refs_9_), channel_id=1, source_target_pairs={{0,24},{8,0},{16,8},{24,16},{1,25},{9,1},{17,9},{25,17},{2,26},{10... | collective-permute-start | bytes 196616 | tf_op jit(solution)/shard_map/ppermute | solution.py:235
  241.7 2.0 copy-start.15
  243.7 0.6 copy-start.24
  252.3 4.9 %copy-start.5 = (f32[384,384]{1,0:T(8,128)S(1)}, f32[384,384]{1,0:T(8,128)}, u32[]{:S(2)}) copy-start(f32[384,384]{1,0:T(8,128)} %fusion.36) | copy-start | bytes 1769476
  252.3 10.5 %all-to-all-start.6 = ((f32[8,16,512]{2,1,0:T(8,128)}), f32[8,16,512]{2,1,0:T(8,128)S(1)}, u32[]{:S(2)}, u32[]{:S(2)}) async-start(f32[8,16,512]{2,1,0:T(8,128)} %bitcast.122), calls=%async_computation.6 | async-start | bytes 524288 | tf_op jit(solution)/shard_map/all_to_all | solution.py:216
  257.3 8.0 %copy-start.6 = (f32[384,384]{1,0:T(8,128)S(1)}, f32[384,384]{1,0:T(8,128)}, u32[]{:S(2)}) copy-start(f32[384,384]{1,0:T(8,128)} %fusion.37) | copy-start | bytes 1769476
  258.7 17.2 %copy-start.2 = (bf16[384,2048]{1,0:T(8,128)(2,1)S(1)}, bf16[384,2048]{1,0:T(8,128)(2,1)}, u32[]{:S(2)}) copy-start(bf16[384,2048]{1,0:T(8,128)(2,1)} %get-tuple-element.92.flat_ref) | copy-start | bytes 4718596
  262.8 6.1 %collective-permute-start.20 = (f32[16,512]{1,0:T(8,128)S(1)}, f32[16,512]{1,0:T(8,128)S(1)}, u32[]{:S(2)}, u32[]{:S(2)}) collective-permute-start(f32[16,512]{1,0:T(8,128)S(1)} %reduce_sum.104), channel_id=1, source_target_pairs={{0,0},{1,8},{2,16},{3,24},{4,1},{5,9},{6,17},{7,25},{8,2},{9,10},{... | collective-permute-start | bytes 98312 | tf_op jit(solution)/shard_map/ppermute | solution.py:228
  269.0 8.6 %copy-start.28 = (f32[16,512]{1,0:T(8,128)}, f32[16,512]{1,0:T(8,128)S(1)}, u32[]{:S(2)}) copy-start(f32[16,512]{1,0:T(8,128)S(1)} %collective-permute-done.20.refs_4_) | copy-start | bytes 98308
  269.0 8.6 %collective-permute-start.21 = (f32[16,512]{1,0:T(8,128)S(1)}, f32[16,512]{1,0:T(8,128)S(1)}, u32[]{:S(2)}, u32[]{:S(2)}) collective-permute-start(f32[16,512]{1,0:T(8,128)S(1)} %collective-permute-done.20.refs_4_), channel_id=1, source_target_pairs={{0,8},{8,16},{16,24},{24,0},{1,9},{9,17},{17,25},{25,1},{2,10},{10... | collective-permute-start | bytes 98312 | tf_op jit(solution)/shard_map/ppermute | solution.py:235
  275.5 2.8 collective-permute-start.22
  275.5 3.3 collective-permute-start.23
  277.6 1.3 copy-start.29
  281.9 2.8 copy-start.1
  281.9 2.8 copy-start.7
  288.3 10.2 %all-to-all-start.7 = ((f32[32,8,128]{2,1,0:T(8,128)}), f32[32,8,128]{2,1,0:T(8,128)S(1)}, u32[]{:S(2)}, u32[]{:S(2)}) async-start(f32[32,8,128]{2,1,0:T(8,128)} %broadcast_in_dim.3), calls=%async_computation.7 | async-start | bytes 262144 | tf_op jit(solution)/shard_map/all_to_all | solution.py:330
  293.8 10.2 %copy-start.4 = (f32[8,48,512]{2,1,0:T(8,128)S(1)}, f32[8,48,512]{2,1,0:T(8,128)}, u32[]{:S(2)}) copy-start(f32[8,48,512]{2,1,0:T(8,128)} %copy-done.3) | copy-start | bytes 2359300
  299.9 23.6 %all-to-all-start.8 = ((f32[8,48,512]{2,1,0:T(8,128)}), f32[8,48,512]{2,1,0:T(8,128)S(1)}, u32[]{:S(2)}, u32[]{:S(2)}) async-start(f32[8,48,512]{2,1,0:T(8,128)} %bitcast.19), calls=%async_computation.8 | async-start | bytes 1572864 | tf_op jit(solution)/shard_map/all_to_all | solution.py:216
  323.6 12.0 %collective-permute-start.24 = (f32[96,512]{1,0:T(8,128)S(1)}, f32[96,512]{1,0:T(8,128)S(1)}, u32[]{:S(2)}, u32[]{:S(2)}) collective-permute-start(f32[96,512]{1,0:T(8,128)S(1)} %pad_maximum_fusion.3), channel_id=1, source_target_pairs={{0,0},{1,8},{2,16},{3,24},{4,1},{5,9},{6,17},{7,25},{8,2},{9,10},{... | collective-permute-start | bytes 589832 | tf_op jit(solution)/shard_map/ppermute | solution.py:228
  335.6 15.2 %collective-permute-start.25 = (f32[96,512]{1,0:T(8,128)S(1)}, f32[96,512]{1,0:T(8,128)S(1)}, u32[]{:S(2)}, u32[]{:S(2)}) collective-permute-start(f32[96,512]{1,0:T(8,128)S(1)} %collective-permute-done.24), channel_id=1, source_target_pairs={{0,8},{8,16},{16,24},{24,0},{1,9},{9,17},{17,25},{25,1},{2,10},{10... | collective-permute-start | bytes 589832 | tf_op jit(solution)/shard_map/ppermute | solution.py:235
  336.3 14.5 %collective-permute-start.26 = (f32[96,512]{1,0:T(8,128)S(1)}, f32[96,512]{1,0:T(8,128)S(1)}, u32[]{:S(2)}, u32[]{:S(2)}) collective-permute-start(f32[96,512]{1,0:T(8,128)S(1)} %collective-permute-done.24), channel_id=1, source_target_pairs={{0,16},{8,24},{16,0},{24,8},{1,17},{9,25},{17,1},{25,9},{2,18},{10... | collective-permute-start | bytes 589832 | tf_op jit(solution)/shard_map/ppermute | solution.py:235
  338.6 12.2 %collective-permute-start.27 = (f32[96,512]{1,0:T(8,128)S(1)}, f32[96,512]{1,0:T(8,128)S(1)}, u32[]{:S(2)}, u32[]{:S(2)}) collective-permute-start(f32[96,512]{1,0:T(8,128)S(1)} %collective-permute-done.24), channel_id=1, source_target_pairs={{0,24},{8,0},{16,8},{24,16},{1,25},{9,1},{17,9},{25,17},{2,26},{10... | collective-permute-start | bytes 589832 | tf_op jit(solution)/shard_map/ppermute | solution.py:235
  351.1 0.9 copy-start.32
  (9 other events, 5.6 us)
